TPU v7x, 128 devices: a whole 4x4x4 slice. The times are simulated.
128 devices in a mesh: batch: 16 (over y, x), tile: 8 (over z, core).
Axes of the slice: x: 4, y: 4, z: 4, core: 2. Of those that a mesh axis runs over, the one named last changes fastest.
Arguments:
- object_field: float32 [2, 2, 6144, 3072], P(None, None, 'batch', 'tile'), may hold values from -6 to 6
- probe_wave: bfloat16 [2, 256, 256], replicated, may hold values from -4.1875 to 4.1875
- intensities: float32 [2048, 256, 256], P(('batch', 'tile')), may hold values from 0 to 4
- owner_rows: int32 [2048, 1], P(('batch', 'tile')), may hold values from 0 to 15; in each aligned block of 16 rows (0 to 15, 16 to 31, ...) at most 2 rows name the same one
- offsets: int32 [2048, 2], P(('batch', 'tile')), may hold values from 0 to 128
Outputs:
- new_object: float32 [2, 2, 6144, 3072], P(None, None, 'batch', 'tile')
- new_probe: float32 [2, 256, 256], replicated
Inputs may be any that keep to these rules, and one draw needn't show every extreme that they name: `owner_rows`: within the 16 positions of one device, each tile row is named at most 2 times.
All inputs are finite; a program needn't handle non-finite values.
Results may differ from a plain program's by a relative error of at most 0.008.
The roundings to bfloat16 on the way count: a program that leaves them out, or rounds other values in their place, can miss the bound.
Values may be sent and summed in bfloat16 or wider, within the bound.
No kernel may reach another device: no remote copies, remote signals or barrier semaphores. Data moves between devices by JAX's collectives and lax.ppermute only.
A program may use at most 192 MiB of HBM per device.

v0:
```python
import jax
import jax.numpy as jnp
import numpy as np
from jax import lax
from jax.experimental import pallas as pl
from jax.experimental.pallas import tpu as pltpu
from jax.sharding import Mesh
from jax.sharding import PartitionSpec as P

BATCH = ("batch_0", "batch_1")
TILE = ("tile_0", "tile_1")
BATCH_TILE = BATCH + TILE

update_rate = 0.1
tv_weight = 12.0
tv_smooth = 1.0
probe_rate = 0.04

N = 256
T = 384
CAP = 2
R = 32
PIECES = N // R
F32 = jnp.float32
BF16 = jnp.bfloat16


def tables():
    counter = np.arange(N)
    angles = (counter[:, None] * counter[None, :] % N) * (2.0 * np.pi / N)
    cos_table = (np.cos(angles) / np.sqrt(N)).astype(jnp.bfloat16)
    sin_table = (-np.sin(angles) / np.sqrt(N)).astype(jnp.bfloat16)
    freq = (counter + N // 2) % N - N // 2
    squared = (freq * freq).astype(np.float64)
    phases = -(0.5 / N) * (squared[:, None] + squared[None, :])
    prop = np.stack([np.cos(phases), np.sin(phases)]).astype(np.float32)
    return np.stack([cos_table, sin_table, -sin_table]), prop


def rows(j):
    return pl.ds(R * j, R)


def issue(acc, regs, pushes, lhs):
    for step in range(2):
        for q in range(2):
            pltpu.matmul_push_rhs(pushes[q][step], staging_register=regs[step], mxu_index=q)
        for j in range(PIECES):
            for q in range(2):
                pltpu.matmul_acc_lhs(
                    acc[q][j], lhs[q][step](j), load_staged_rhs=regs[step] if j == 0 else None
                )


def multislice_steps(env, start, scale, slot_index, acc, x, y, psi, trans, field):
    tile, probe, ints, tab, prop, probe_sum = env
    row, col = start
    regs = (0, 1)
    lane = lax.broadcasted_iota(jnp.int32, (R, 128), 1)
    back = (128 - col) & 127
    forth = col & 127
    keep = lane < 128 - col
    moved = lane >= col

    def left(forward):
        sin, neg = (1, 2) if forward else (2, 1)
        xr, xi = x[0], x[1]
        issue(
            acc,
            regs,
            ((xr[...], xi[...]), (xr[...], xi[...])),
            (
                (lambda j: tab[0, rows(j)], lambda j: tab[neg, rows(j)]),
                (lambda j: tab[sin, rows(j)], lambda j: tab[0, rows(j)]),
            ),
        )

    def middle():
        for j in range(PIECES):
            for q in range(2):
                y[q][rows(j)] = pltpu.matmul_pop(acc[q][j]).astype(BF16)

    def right(forward):
        sin, neg = (1, 2) if forward else (2, 1)
        lhs = (lambda j: y[0][rows(j)], lambda j: y[1][rows(j)])
        issue(acc, regs, ((tab[0], tab[neg]), (tab[sin], tab[0])), (lhs, lhs))

    def pops(j):
        return pltpu.matmul_pop(acc[0][j]), pltpu.matmul_pop(acc[1][j])

    def cut(s, q, j):
        at = pl.ds(row + R * j, R)
        turned = [pltpu.roll(tile[s, q, k, at, :], back, 1) for k in range(3)]
        return jnp.concatenate(
            [jnp.where(keep, turned[0], turned[1]), jnp.where(keep, turned[1], turned[2])], 1
        )

    def put(s, q, j, value):
        value = value.astype(BF16).astype(F32)
        turned = [pltpu.roll(value[:, 128 * k : 128 * k + 128], forth, 1) for k in range(2)]
        parts = (
            jnp.where(moved, turned[0], 0.0),
            jnp.where(moved, turned[1], turned[0]),
            jnp.where(moved, 0.0, turned[1]),
        )
        at = pl.ds(row + R * j, R)
        for k in range(3):
            field[s, q, k, at, :] = field[s, q, k, at, :] + parts[k]

    def product(s, wave):
        for j in range(PIECES):
            tr, ti = cut(s, 0, j), cut(s, 1, j)
            trans[s, 0, rows(j)] = tr
            trans[s, 1, rows(j)] = ti
            pr, pi = wave[0, rows(j)].astype(F32), wave[1, rows(j)].astype(F32)
            x[0][rows(j)] = (pr * tr - pi * ti).astype(BF16)
            x[1][rows(j)] = (pr * ti + pi * tr).astype(BF16)

    def kick(sign):
        for j in range(PIECES):
            fr, fi = pops(j)
            hr, hi = prop[0, rows(j)], prop[1, rows(j)]
            if sign > 0:
                x[0][rows(j)] = (hr * fr - hi * fi).astype(BF16)
                x[1][rows(j)] = (hr * fi + hi * fr).astype(BF16)
            else:
                x[0][rows(j)] = (hr * fr + hi * fi).astype(BF16)
                x[1][rows(j)] = (hr * fi - hi * fr).astype(BF16)

    product(0, probe)
    yield
    left(True)
    yield
    middle()
    right(True)
    yield
    kick(1)
    left(False)
    yield
    middle()
    right(False)
    yield
    for j in range(PIECES):
        wr, wi = pops(j)
        wr, wi = wr.astype(BF16), wi.astype(BF16)
        psi[0, rows(j)] = wr
        psi[1, rows(j)] = wi
        wr, wi = wr.astype(F32), wi.astype(F32)
        tr, ti = cut(1, 0, j), cut(1, 1, j)
        trans[1, 0, rows(j)] = tr
        trans[1, 1, rows(j)] = ti
        x[0][rows(j)] = (wr * tr - wi * ti).astype(BF16)
        x[1][rows(j)] = (wr * ti + wi * tr).astype(BF16)
    left(True)
    yield
    middle()
    right(True)
    yield
    for j in range(PIECES):
        er, ei = pops(j)
        misfit = scale * (er * er + ei * ei - ints[slot_index, rows(j)].astype(F32))
        x[0][rows(j)] = (misfit * er).astype(BF16)
        x[1][rows(j)] = (misfit * ei).astype(BF16)
    left(False)
    yield
    middle()
    right(False)
    yield
    for j in range(PIECES):
        gr, gi = pops(j)
        wr, wi = psi[0, rows(j)].astype(F32), psi[1, rows(j)].astype(F32)
        tr, ti = trans[1, 0, rows(j)], trans[1, 1, rows(j)]
        x[0][rows(j)] = (gr * tr + gi * ti).astype(BF16)
        x[1][rows(j)] = (gi * tr - gr * ti).astype(BF16)
        put(1, 0, j, gr * wr + gi * wi)
        put(1, 1, j, gi * wr - gr * wi)
    left(False)
    yield
    middle()
    right(False)
    yield
    kick(-1)
    left(True)
    yield
    middle()
    right(True)
    yield
    for j in range(PIECES):
        gr, gi = pops(j)
        wr, wi = probe[0, rows(j)].astype(F32), probe[1, rows(j)].astype(F32)
        tr, ti = trans[0, 0, rows(j)], trans[0, 1, rows(j)]
        probe_sum[0, rows(j)] = probe_sum[0, rows(j)] + (gr * tr + gi * ti)
        probe_sum[1, rows(j)] = probe_sum[1, rows(j)] + (gi * tr - gr * ti)
        put(0, 0, j, gr * wr + gi * wi)
        put(0, 1, j, gi * wr - gr * wi)


def multislice_kernel(
    meta, tile_in, base, probe, ints, tab, prop, field_out, probe_sum, tile, field_a, field_b, *work
):
    xa, xb, ya, yb, psi_a, psi_b, trans_a, trans_b = work
    for s in range(2):
        for q in range(2):
            for k in range(3):
                at = pl.ds(128 * k, 128)
                tile[s, q, k] = tile_in[s, q, :, at].astype(BF16).astype(F32)
                field_a[s, q, k] = jnp.zeros((T, 128), F32)
                field_b[s, q, k] = jnp.zeros((T, 128), F32)
    probe_sum[...] = jnp.zeros((2, N, N), F32)
    count = meta[0]
    env = (tile, probe, ints, tab, prop, probe_sum)

    def body(acc_a, acc_b):
        for one in acc_a + acc_b:
            for ref in one:
                pltpu.matmul_pop(ref)

        @pl.loop(0, (count + 1) // 2)
        def _(pair):
            ia = 2 * pair
            there = ia + 1 < count
            ib = jnp.where(there, ia + 1, ia)
            sa, sb = meta[8 + 4 * ia], meta[8 + 4 * ib]
            at_a = (meta[9 + 4 * ia], meta[10 + 4 * ia])
            at_b = (meta[9 + 4 * ib], meta[10 + 4 * ib])
            steps_a = multislice_steps(
                env, at_a, F32(0.5), sa, acc_a, (xa.at[0], xa.at[1]), (ya.at[0], ya.at[1]), psi_a, trans_a, field_a
            )
            steps_b = multislice_steps(
                env,
                at_b,
                jnp.where(there, F32(0.5), F32(0.0)),
                sb,
                acc_b,
                (xb.at[0], xb.at[1]),
                (yb.at[0], yb.at[1]),
                psi_b,
                trans_b,
                field_b,
            )
            live = [steps_a, steps_b]
            while live:
                for one in list(live):
                    if next(one, 1) == 1:
                        live.remove(one)

    refs = tuple(tuple(pltpu.ACC(q)((R, N), F32) for _ in range(PIECES)) for q in range(2))
    pl.run_scoped(body, refs, refs)
    for s in range(2):
        for q in range(2):
            for k in range(3):
                at = pl.ds(128 * k, 128)
                grad = field_a[s, q, k] + field_b[s, q, k]
                field_out[s, q, :, at] = base[s, q, :, at] - update_rate * grad


def multislice_call(meta, tile, base, probe, ints):
    tab, prop = tables()
    vmem = pl.BlockSpec(memory_space=pltpu.VMEM)
    wide = pltpu.VMEM((2, 2, 3, T, 128), F32)
    small = pltpu.VMEM((2, N, N), BF16)
    return pl.pallas_call(
        multislice_kernel,
        out_shape=(jax.ShapeDtypeStruct((2, 2, T, T), F32), jax.ShapeDtypeStruct((2, N, N), F32)),
        in_specs=[pl.BlockSpec(memory_space=pltpu.SMEM)] + [vmem] * 6,
        out_specs=(vmem, vmem),
        scratch_shapes=[wide, wide, wide] + [small] * 6 + [pltpu.VMEM((2, 2, N, N), F32)] * 2,
        compiler_params=pltpu.CompilerParams(vmem_limit_bytes=60 << 20),
        name="multislice",
    )(meta, tile, base, probe, ints, tab, prop)


def pack_kernel(slots, values, out):
    out[...] = values[...].astype(BF16)


def pack_call(slots, intensities):
    count = intensities.shape[0]
    return pl.pallas_call(
        pack_kernel,
        out_shape=jax.ShapeDtypeStruct((count * CAP, N, N), BF16),
        grid_spec=pltpu.PrefetchScalarGridSpec(
            num_scalar_prefetch=1,
            grid=(count,),
            in_specs=[pl.BlockSpec((1, N, N), lambda i, slots: (i, 0, 0))],
            out_specs=pl.BlockSpec((1, N, N), lambda i, slots: (slots[i], 0, 0)),
        ),
        name="pack",
    )(slots, intensities)


def extended(x, sides, width):
    for axis, dim in sides:
        size, length = (lax.axis_size(axis), x.shape[dim])
        up = [(i, (i + 1) % size) for i in range(size)]
        down = [(j, i) for i, j in up]
        last = lax.slice_in_dim(x, length - width, length, axis=dim)
        first = lax.slice_in_dim(x, 0, width, axis=dim)
        before = lax.ppermute(last, axis, up)
        after = lax.ppermute(first, axis, down)
        x = jnp.concatenate([before, x, after], axis=dim)
    return x


def tv_local(padded):
    corner_cells = padded[:, :, :-1, :-1]
    down_diff = padded[:, :, 1:, :-1] - corner_cells
    right_diff = padded[:, :, :-1, 1:] - corner_cells
    weight = 1.0 / jnp.sqrt(
        jnp.sum(down_diff * down_diff + right_diff * right_diff, axis=1, keepdims=True) + tv_smooth
    )
    flow_down = weight * down_diff
    flow_right = weight * right_diff
    return (
        flow_down[:, :, :-1, 1:]
        + flow_right[:, :, 1:, :-1]
        - flow_down[:, :, 1:, 1:]
        - flow_right[:, :, 1:, 1:]
    )


def on_device(object_field, probe_wave, intensities, owner_rows, offsets):
    local_rows = intensities.shape[0]
    nbatch = lax.axis_size(BATCH)
    slots_all = nbatch * CAP
    targets = owner_rows[:, 0]
    serial = jnp.arange(local_rows, dtype=jnp.int32)
    earlier = (targets[:, None] == targets[None, :]) & (serial[None, :] < serial[:, None])
    slot_of = targets * CAP + jnp.sum(earlier.astype(jnp.int32), axis=1)
    hit = slot_of[:, None] == jnp.arange(slots_all, dtype=jnp.int32)[None, :]
    request = jnp.sum(jnp.where(hit[:, :, None], offsets[:, None, :] + 1, 0), axis=0)
    wanted = lax.all_to_all(
        request.reshape(nbatch, CAP * 2), BATCH, split_axis=0, concat_axis=0, tiled=True
    ).reshape(slots_all, 2)
    sent = pack_call(slot_of, intensities).reshape(nbatch, CAP, N, N)
    ints = lax.all_to_all(sent, BATCH, split_axis=0, concat_axis=0, tiled=True)
    ints = ints.reshape(slots_all, N, N)
    used = (wanted[:, 0] > 0).astype(jnp.int32)
    place = jnp.cumsum(used) - used
    order = jnp.arange(slots_all, dtype=jnp.int32)
    takes = (place[None, :] == order[:, None]) & (used[None, :] > 0)
    fields = jnp.stack([order, wanted[:, 0] - 1, wanted[:, 1] - 1, order], 1)
    listed = jnp.sum(jnp.where(takes[:, :, None], fields[None], 0), axis=1)
    head = jnp.full((8,), jnp.sum(used), jnp.int32)
    meta = jnp.concatenate([head, listed.reshape(-1)])
    padded = extended(object_field, ((BATCH, 2), (TILE, 3)), 1)
    base = object_field - (update_rate * tv_weight) * tv_local(padded)
    new_object, probe_local = multislice_call(meta, object_field, base, probe_wave, ints)
    probe_total = lax.psum(probe_local, BATCH_TILE)
    new_probe = probe_wave.astype(F32) - probe_rate * probe_total
    return (new_object, new_probe)


def solution(mesh):
    finer = Mesh(mesh.devices.reshape(4, 4, 4, 2), ("batch_0", "batch_1", "tile_0", "tile_1"))
    placed = (P(None, None, BATCH, TILE), P(), P(BATCH_TILE), P(BATCH_TILE), P(BATCH_TILE))
    return jax.shard_map(
        on_device,
        mesh=finer,
        in_specs=placed,
        out_specs=(P(None, None, BATCH, TILE), P()),
        check_vma=False,
    )
```

profile of v0, /device:TPU:1, one launch (start us, length us, event | category | flops | bytes accessed | tf_op | source)
XLA Modules:
  0.0 350.4 jit_solution(15360655184496452627)
XLA Ops:
  7.2 0.9 convert_reduce_fusion.1
  8.8 0.7 broadcast_add_fusion
  9.7 0.7 all_to_all.9
  10.3 7.6 %all-to-all-start = ((s32[16,1,4]{2,1,0:T(1,128)}), s32[16,1,4]{2,1,0:T(1,128)S(1)}, u32[]{:S(2)}, u32[]{:S(2)}) async-start(s32[16,1,4]{2,1,0:T(1,128)} %bitcast.3), calls=%async_computation | async-start | bytes 16384 | tf_op jit(solution)/shard_map/all_to_all | solution.py:332
  17.9 1.2 multiply_add_fusion.slots
  19.1 10.5 %pack.1 = bf16[32,256,256]{2,1,0:T(8,128)(2,1)} custom-call(s32[16]{0:T(128)} %multiply_add_fusion.slots, f32[16,256,256]{2,1,0:T(8,128)} %values.1), custom_call_target="tpu_custom_call" | custom-call | tf_op jit(solution)/shard_map/pack/pallas_call | solution.py:279
  29.6 6.8 %all-to-all-start.1 = ((bf16[16,2,256,256]{3,2,1,0:T(8,128)(2,1)}), bf16[16,2,256,256]{3,2,1,0:T(8,128)(2,1)}, u32[]{:S(2)}, u32[]{:S(2)}) async-start(bf16[16,2,256,256]{3,2,1,0:T(8,128)(2,1)} %bitcast.11), calls=%async_computation.1 | async-start | bytes 8388608 | tf_op jit(solution)/shard_map/all_to_all | solution.py:336
  36.4 1.4 collective-permute-start
  37.8 3.5 collective-permute-start.1
  41.8 0.7 reduce.8
  43.6 46.5 %collective-permute-done = f32[2,2,1,384]{3,2,1,0:T(1,128)S(1)} collective-permute-done((f32[2,2,1,384]{3,2,1,0:T(1,128)S(1)}, f32[2,2,1,384]{3,2,1,0:T(1,128)S(1)}, u32[]{:S(2)}, u32[]{:S(2)}) %collective-permute-start) | collective-permute-done | bytes 6176 | tf_op jit(solution)/shard_map/ppermute | solution.py:299
  90.2 5.8 %collective-permute-done.1 = f32[2,2,1,384]{3,2,1,0:T(1,128)S(1)} collective-permute-done((f32[2,2,1,384]{3,2,1,0:T(1,128)S(1)}, f32[2,2,1,384]{3,2,1,0:T(1,128)S(1)}, u32[]{:S(2)}, u32[]{:S(2)}) %collective-permute-start.1) | collective-permute-done | bytes 6176 | tf_op jit(solution)/shard_map/ppermute | solution.py:300
  96.0 1.2 pad_maximum_fusion.3
  97.1 1.5 copy.24
  98.6 3.7 %collective-permute-start.2 = (f32[2,2,386,1]{2,1,3,0:T(2,128)S(1)}, f32[2,2,386,1]{2,1,3,0:T(2,128)S(1)}, u32[]{:S(2)}, u32[]{:S(2)}) collective-permute-start(f32[2,2,386,1]{2,1,3,0:T(2,128)S(1)} %copy.24), channel_id=1, source_target_pairs={{0,1},{1,2},{2,3},{3,4},{4,5},{5,6},{6,7},{7,0},{8,9},{9,10},{10,1... | collective-permute-start | bytes 18536 | tf_op jit(solution)/shard_map/ppermute | solution.py:299
  103.0 1.3 concatenate.14.meta
  104.3 1.2 copy.25
  106.0 2.2 maximum_maximum_fusion
  108.2 1.4 add_reduce_fusion
  109.8 1.1 broadcast_multiply_fusion.1
  110.9 3.6 %fusion.2.base = f32[2,2,384,384]{3,2,1,0:T(8,128)} fusion(f32[2,2,384,384]{3,2,1,0:T(8,128)S(1)} %copy-done, f32[2,2,385,385]{3,2,1,0:T(8,128)S(1)} %get-tuple-element.11, f32[2,2,385,385]{3,2,1,0:T(8,128)S(1)} %get-tuple-element.10), kind=kLoop, calls=%fused_computation.9 | loop fusion | flops 2949120 | bytes 14155776 | tf_op jit(solution)/shard_map/sub | solution.py:347
  114.5 39.5 %multislice.1 = (f32[2,2,384,384]{3,2,1,0:T(8,128)}, f32[2,256,256]{2,1,0:T(8,128)}) custom-call(s32[136]{0:T(256)} %concatenate.14.meta, f32[2,2,384,384]{3,2,1,0:T(8,128)} %tile_in.1, f32[2,2,384,384]{3,2,1,0:T(8,128)} %fusion.2.base, bf16[2,256,256]{2,1,0:T(8,128)(2,1)} %probe.1, bf16[32,256,256]{2,1,0:T(8,128)(2,1)} %bitcast.5.ints, ...), custom_call_target="tpu_custom_call" | custom-call | tf_op jit(solution)/shard_map/multislice/pallas_call | solution.py:262
  154.0 187.7 %all-reduce.3.cloned.1.call-done = f32[2,256,256]{2,1,0:T(8,128)} async-done(((f32[2,256,256]{2,1,0:T(8,128)}), f32[2,256,256]{2,1,0:T(8,128)}) %all-reduce.3.cloned.1.call-update) | async-done | bytes 524304 | tf_op jit(solution)/shard_map/psum | solution.py:349
  341.6 1.9 multiply_subtract_fusion
  (33 shorter events, 4.1 us)
Async XLA Ops:
  10.3 19.2 %all-to-all-start = ((s32[16,1,4]{2,1,0:T(1,128)}), s32[16,1,4]{2,1,0:T(1,128)S(1)}, u32[]{:S(2)}, u32[]{:S(2)}) async-start(s32[16,1,4]{2,1,0:T(1,128)} %bitcast.3), calls=%async_computation | async-start | bytes 16384 | tf_op jit(solution)/shard_map/all_to_all | solution.py:332
  29.6 6.9 %copy-start = (f32[2,2,384,384]{3,2,1,0:T(8,128)S(1)}, f32[2,2,384,384]{3,2,1,0:T(8,128)}, u32[]{:S(2)}) copy-start(f32[2,2,384,384]{3,2,1,0:T(8,128)} %tile_in.1) | copy-start | bytes 7077892
  29.6 84.9 %all-to-all-start.1 = ((bf16[16,2,256,256]{3,2,1,0:T(8,128)(2,1)}), bf16[16,2,256,256]{3,2,1,0:T(8,128)(2,1)}, u32[]{:S(2)}, u32[]{:S(2)}) async-start(bf16[16,2,256,256]{3,2,1,0:T(8,128)(2,1)} %bitcast.11), calls=%async_computation.1 | async-start | bytes 8388608 | tf_op jit(solution)/shard_map/all_to_all | solution.py:336
  36.4 305.2 %all-reduce.3.cloned.1.call-start = ((), (), s32[]{:S(2)}) async-start(), calls=%async_computation.2 | async-start | bytes 1048576 | tf_op jit(solution)/shard_map/psum | solution.py:349
  36.4 53.7 %collective-permute-start = (f32[2,2,1,384]{3,2,1,0:T(1,128)S(1)}, f32[2,2,1,384]{3,2,1,0:T(1,128)S(1)}, u32[]{:S(2)}, u32[]{:S(2)}) collective-permute-start(f32[2,2,1,384]{3,2,1,0:T(1,128)S(1)} %get-tuple-element.14), channel_id=1, source_target_pairs={{0,8},{8,16},{16,24},{24,32},{32,40},{40,48},{48,56},{56,64},{64,7... | collective-permute-start | bytes 18440 | tf_op jit(solution)/shard_map/ppermute | solution.py:299
  37.8 58.1 %collective-permute-start.1 = (f32[2,2,1,384]{3,2,1,0:T(1,128)S(1)}, f32[2,2,1,384]{3,2,1,0:T(1,128)S(1)}, u32[]{:S(2)}, u32[]{:S(2)}) collective-permute-start(f32[2,2,1,384]{3,2,1,0:T(1,128)S(1)} %get-tuple-element.15), channel_id=1, source_target_pairs={{8,0},{16,8},{24,16},{32,24},{40,32},{48,40},{56,48},{64,56},{72,6... | collective-permute-start | bytes 18440 | tf_op jit(solution)/shard_map/ppermute | solution.py:300
  98.6 5.6 %collective-permute-start.2 = (f32[2,2,386,1]{2,1,3,0:T(2,128)S(1)}, f32[2,2,386,1]{2,1,3,0:T(2,128)S(1)}, u32[]{:S(2)}, u32[]{:S(2)}) collective-permute-start(f32[2,2,386,1]{2,1,3,0:T(2,128)S(1)} %copy.24), channel_id=1, source_target_pairs={{0,1},{1,2},{2,3},{3,4},{4,5},{5,6},{6,7},{7,0},{8,9},{9,10},{10,1... | collective-permute-start | bytes 18536 | tf_op jit(solution)/shard_map/ppermute | solution.py:299
  102.6 3.1 collective-permute-start.3
  114.5 227.2 %copy-start.1 = (bf16[2,256,256]{2,1,0:T(8,128)(2,1)S(1)}, bf16[2,256,256]{2,1,0:T(8,128)(2,1)}, u32[]{:S(2)}) copy-start(bf16[2,256,256]{2,1,0:T(8,128)(2,1)} %probe.1) | copy-start | bytes 786436
Sparse Core Ops, SparseCore 0:
  154.1 187.4 all-reduce.2
where the time goes:
time: 350 us
  waiting for transfers between devices  240 us (69%)
  Pallas kernels  49.9 us (14%)
  starting transfers between devices  22.9 us (7%)
  other arithmetic  16.9 us (5%)
  between operations  14.1 us (4%)
  local copies, waits for them, and re-layouts  6.24 us (2%)
    psum x1, waiting for transfers between devices, on_device(): probe_total = lax.psum(probe_local, BATCH_TILE)  188 us
    ppermute x2, waiting for transfers between devices, extended(): before = lax.ppermute(last, axis, up)  46.5 us
    pallas_call x1, Pallas kernels, multislice_call(): pl.pallas_call(multislice_kernel, out_shape=(jax.ShapeDtypeStruct((2, 2,...  39.5 us
    pallas_call x1, Pallas kernels, pack_call(): pl.pallas_call(pack_kernel, out_shape=jax.ShapeDtypeStruct((count * CAP,...  10.5 us
    all_to_all x1, starting transfers between devices, on_device(): lax.all_to_all(request.reshape(nbatch, CAP * 2), BATCH, split_axis=0, con...  7.57 us
  transfers between devices with their start and end apart: 7, of which 4 were waited for; matrix products, arithmetic and copies ran while one was open for 5% of the time, Pallas kernels for 3%

commit v1 on v0

v1 whole, which is shorter than its diff:
```python
import jax
import jax.numpy as jnp
import numpy as np
from jax import lax
from jax.experimental import pallas as pl
from jax.experimental.pallas import tpu as pltpu
from jax.sharding import Mesh
from jax.sharding import PartitionSpec as P

BATCH = ("batch_0", "batch_1")
TILE = ("tile_0", "tile_1")
BATCH_TILE = BATCH + TILE

update_rate = 0.1
tv_weight = 12.0
tv_smooth = 1.0
probe_rate = 0.04

N = 256
T = 384
CAP = 2
R = 32
PIECES = N // R
F32 = jnp.float32
BF16 = jnp.bfloat16


def tables():
    counter = np.arange(N)
    angles = (counter[:, None] * counter[None, :] % N) * (2.0 * np.pi / N)
    cos_table = (np.cos(angles) / np.sqrt(N)).astype(jnp.bfloat16)
    sin_table = (-np.sin(angles) / np.sqrt(N)).astype(jnp.bfloat16)
    freq = (counter + N // 2) % N - N // 2
    squared = (freq * freq).astype(np.float64)
    phases = -(0.5 / N) * (squared[:, None] + squared[None, :])
    prop = np.stack([np.cos(phases), np.sin(phases)]).astype(np.float32)
    return np.stack([cos_table, sin_table, -sin_table]), prop


def rows(j):
    return pl.ds(R * j, R)


def issue(acc, regs, pushes, lhs):
    for step in range(2):
        for q in range(2):
            pltpu.matmul_push_rhs(pushes[q][step], staging_register=regs[step], mxu_index=q)
        for j in range(PIECES):
            for q in range(2):
                pltpu.matmul_acc_lhs(
                    acc[q][j], lhs[q][step](j), load_staged_rhs=regs[step] if j == 0 else None
                )


def shared(start, acc, x, y, tab):
    row, col = start
    regs = (0, 1)
    lane = lax.broadcasted_iota(jnp.int32, (R, 128), 1)
    back = (128 - col) & 127
    forth = col & 127
    keep = lane < 128 - col
    moved = lane >= col

    def left(forward):
        sin, neg = (1, 2) if forward else (2, 1)
        xr, xi = x[0], x[1]
        issue(
            acc,
            regs,
            ((xr[...], xi[...]), (xr[...], xi[...])),
            (
                (lambda j: tab[0, rows(j)], lambda j: tab[neg, rows(j)]),
                (lambda j: tab[sin, rows(j)], lambda j: tab[0, rows(j)]),
            ),
        )

    def middle():
        for j in range(PIECES):
            for q in range(2):
                y[q][rows(j)] = pltpu.matmul_pop(acc[q][j]).astype(BF16)

    def right(forward):
        sin, neg = (1, 2) if forward else (2, 1)
        lhs = (lambda j: y[0][rows(j)], lambda j: y[1][rows(j)])
        issue(acc, regs, ((tab[0], tab[neg]), (tab[sin], tab[0])), (lhs, lhs))

    def pops(j):
        return pltpu.matmul_pop(acc[0][j]), pltpu.matmul_pop(acc[1][j])

    def cut(tile, s, q, j):
        at = pl.ds(row + R * j, R)
        turned = [pltpu.roll(tile[s, q, k, at, :], back, 1) for k in range(3)]
        return jnp.concatenate(
            [jnp.where(keep, turned[0], turned[1]), jnp.where(keep, turned[1], turned[2])], 1
        )

    def put(field, s, q, j, value):
        value = value.astype(BF16).astype(F32)
        turned = [pltpu.roll(value[:, 128 * k : 128 * k + 128], forth, 1) for k in range(2)]
        parts = (
            jnp.where(moved, turned[0], 0.0),
            jnp.where(moved, turned[1], turned[0]),
            jnp.where(moved, 0.0, turned[1]),
        )
        at = pl.ds(row + R * j, R)
        for k in range(3):
            field[s, q, k, at, :] = field[s, q, k, at, :] + parts[k]

    def kick(prop, sign):
        for j in range(PIECES):
            fr, fi = pops(j)
            hr, hi = prop[0, rows(j)], prop[1, rows(j)]
            if sign > 0:
                x[0][rows(j)] = (hr * fr - hi * fi).astype(BF16)
                x[1][rows(j)] = (hr * fi + hi * fr).astype(BF16)
            else:
                x[0][rows(j)] = (hr * fr + hi * fi).astype(BF16)
                x[1][rows(j)] = (hr * fi - hi * fr).astype(BF16)

    return left, middle, right, pops, cut, put, kick


def forward_steps(env, start, acc, x, y, psi, exits):
    tile, probe, tab, prop = env
    left, middle, right, pops, cut, _, kick = shared(start, acc, x, y, tab)
    for j in range(PIECES):
        tr, ti = cut(tile, 0, 0, j), cut(tile, 0, 1, j)
        pr, pi = probe[0, rows(j)].astype(F32), probe[1, rows(j)].astype(F32)
        x[0][rows(j)] = (pr * tr - pi * ti).astype(BF16)
        x[1][rows(j)] = (pr * ti + pi * tr).astype(BF16)
    left(True)
    yield
    middle()
    right(True)
    yield
    kick(prop, 1)
    left(False)
    yield
    middle()
    right(False)
    yield
    for j in range(PIECES):
        wr, wi = pops(j)
        wr, wi = wr.astype(BF16), wi.astype(BF16)
        psi[0, rows(j)] = wr
        psi[1, rows(j)] = wi
        wr, wi = wr.astype(F32), wi.astype(F32)
        tr, ti = cut(tile, 1, 0, j), cut(tile, 1, 1, j)
        x[0][rows(j)] = (wr * tr - wi * ti).astype(BF16)
        x[1][rows(j)] = (wr * ti + wi * tr).astype(BF16)
    left(True)
    yield
    middle()
    right(True)
    yield
    for j in range(PIECES):
        er, ei = pops(j)
        exits[0, rows(j)] = er
        exits[1, rows(j)] = ei


def backward_steps(env, start, scale, ints, acc, x, y, psi, exits, field):
    tile, probe, tab, prop, probe_sum = env
    left, middle, right, pops, cut, put, kick = shared(start, acc, x, y, tab)
    for j in range(PIECES):
        er, ei = exits[0, rows(j)], exits[1, rows(j)]
        misfit = scale * (er * er + ei * ei - ints[rows(j)].astype(F32))
        x[0][rows(j)] = (misfit * er).astype(BF16)
        x[1][rows(j)] = (misfit * ei).astype(BF16)
    left(False)
    yield
    middle()
    right(False)
    yield
    for j in range(PIECES):
        gr, gi = pops(j)
        wr, wi = psi[0, rows(j)].astype(F32), psi[1, rows(j)].astype(F32)
        tr, ti = cut(tile, 1, 0, j), cut(tile, 1, 1, j)
        x[0][rows(j)] = (gr * tr + gi * ti).astype(BF16)
        x[1][rows(j)] = (gi * tr - gr * ti).astype(BF16)
        put(field, 1, 0, j, gr * wr + gi * wi)
        put(field, 1, 1, j, gi * wr - gr * wi)
    left(False)
    yield
    middle()
    right(False)
    yield
    kick(prop, -1)
    left(True)
    yield
    middle()
    right(True)
    yield
    for j in range(PIECES):
        gr, gi = pops(j)
        wr, wi = probe[0, rows(j)].astype(F32), probe[1, rows(j)].astype(F32)
        tr, ti = cut(tile, 0, 0, j), cut(tile, 0, 1, j)
        probe_sum[0, rows(j)] = probe_sum[0, rows(j)] + (gr * tr + gi * ti)
        probe_sum[1, rows(j)] = probe_sum[1, rows(j)] + (gi * tr - gr * ti)
        put(field, 0, 0, j, gr * wr + gi * wi)
        put(field, 0, 1, j, gi * wr - gr * wi)


def interleave(*steps):
    live = list(steps)
    while live:
        for one in list(live):
            if next(one, 1) == 1:
                live.remove(one)


def list_used(wanted, listed, rank):
    def one(k, used):
        listed[used] = k
        return used + (wanted[2 * CAP * k + 2 * rank] > 0).astype(jnp.int32)

    return lax.fori_loop(0, SOURCES, one, jnp.int32(0))


def chosen(wanted, listed, count, pair, rank):
    there = 2 * pair + 1 < count
    slots = listed[2 * pair], listed[jnp.where(there, 2 * pair + 1, 2 * pair)]
    at = [2 * CAP * k + 2 * rank for k in slots]
    return slots, [(wanted[a] - 1, wanted[a + 1] - 1) for a in at], there


def round_tile(tile_in, tile):
    for s in range(2):
        for q in range(2):
            for k in range(3):
                tile[s, q, k] = tile_in[s, q, :, pl.ds(128 * k, 128)].astype(BF16).astype(F32)


def with_accumulators(body):
    def start(acc_a, acc_b):
        for one in acc_a + acc_b:
            for ref in one:
                pltpu.matmul_pop(ref)
        body(acc_a, acc_b)

    refs = tuple(tuple(pltpu.ACC(q)((R, N), F32) for _ in range(PIECES)) for q in range(2))
    pl.run_scoped(start, refs, refs)


def forward_kernel(rank, wanted, tile_in, probe, tab, prop, exits_out, psi_out, tile, listed, x, y, exits, psi, sems):
    round_tile(tile_in, tile)
    env = (tile, probe, tab, prop)

    def copies(b, at):
        return (
            pltpu.make_async_copy(exits.at[b], exits_out.at[at], sems.at[0, b]),
            pltpu.make_async_copy(psi.at[b], psi_out.at[at], sems.at[1, b]),
        )

    count = list_used(wanted, listed, rank)
    pairs = (count + 1) // 2

    def body(acc_a, acc_b):
        @pl.loop(0, pairs)
        def _(pair):
            b = pair % 2
            _, at, _ = chosen(wanted, listed, count, pair, rank)

            @pl.when(pair >= 2)
            def _():
                for one in copies(b, pair - 2):
                    one.wait()

            interleave(
                *[
                    forward_steps(
                        env,
                        at[i],
                        (acc_a, acc_b)[i],
                        (x.at[i, 0], x.at[i, 1]),
                        (y.at[i, 0], y.at[i, 1]),
                        psi.at[b, i],
                        exits.at[b, i],
                    )
                    for i in range(2)
                ]
            )
            for one in copies(b, pair):
                one.start()

        for late in (2, 1):

            @pl.when(pairs >= late)
            def _():
                for one in copies((pairs - late) % 2, pairs - late):
                    one.wait()

    with_accumulators(body)


def backward_kernel(rank, *refs):
    wanted, tile_in, probe, tab, prop, ints, exits_in, psi_in = refs[:8]
    refs = refs[8:]
    if rank:
        (field_in, probe_in), refs = refs[:2], refs[2:]
    field_out, probe_sum, tile, field_a, field_b, listed, x, y, exits, psi, sems = refs
    count = list_used(wanted, listed, rank)
    pairs = (count + 1) // 2

    def copies(b, at):
        return (
            pltpu.make_async_copy(exits_in.at[at], exits.at[b], sems.at[0, b]),
            pltpu.make_async_copy(psi_in.at[at], psi.at[b], sems.at[1, b]),
        )

    @pl.when(pairs > 0)
    def _():
        for one in copies(0, 0):
            one.start()

    round_tile(tile_in, tile)
    for s in range(2):
        for q in range(2):
            for k in range(3):
                at = pl.ds(128 * k, 128)
                field_a[s, q, k] = field_in[s, q, :, at] if rank else jnp.zeros((T, 128), F32)
                field_b[s, q, k] = jnp.zeros((T, 128), F32)
    probe_sum[...] = probe_in[...] if rank else jnp.zeros((2, N, N), F32)
    env = (tile, probe, tab, prop, probe_sum)

    def body(acc_a, acc_b):
        @pl.loop(0, pairs)
        def _(pair):
            b = pair % 2
            slots, at, there = chosen(wanted, listed, count, pair, rank)

            @pl.when(pair + 1 < pairs)
            def _():
                for one in copies(1 - b, pair + 1):
                    one.start()

            for one in copies(b, pair):
                one.wait()
            scales = F32(0.5), jnp.where(there, F32(0.5), F32(0.0))
            interleave(
                *[
                    backward_steps(
                        env,
                        at[i],
                        scales[i],
                        ints.at[slots[i]],
                        (acc_a, acc_b)[i],
                        (x.at[i, 0], x.at[i, 1]),
                        (y.at[i, 0], y.at[i, 1]),
                        psi.at[b, i],
                        exits.at[b, i],
                        (field_a, field_b)[i],
                    )
                    for i in range(2)
                ]
            )

    with_accumulators(body)
    for s in range(2):
        for q in range(2):
            for k in range(3):
                field_out[s, q, :, pl.ds(128 * k, 128)] = field_a[s, q, k] + field_b[s, q, k]


VMEM = pl.BlockSpec(memory_space=pltpu.VMEM)
SMEM = pl.BlockSpec(memory_space=pltpu.SMEM)
ANY = pl.BlockSpec(memory_space=pl.ANY)
SOURCES = 16
PAIRS = SOURCES // 2
WIDE = pltpu.VMEM((2, 2, 3, T, 128), F32)
PER_PAIR = [
    pltpu.VMEM((2, 2, N, N), BF16),
    pltpu.VMEM((2, 2, N, N), BF16),
    pltpu.VMEM((2, 2, 2, N, N), F32),
    pltpu.VMEM((2, 2, 2, N, N), BF16),
    pltpu.SemaphoreType.DMA((2, 2)),
]
LISTED = pltpu.SMEM((SOURCES + 1,), jnp.int32)


def params(positions, steps):
    flops = positions * steps * 2 * 8 * N**3
    return dict(
        compiler_params=pltpu.CompilerParams(vmem_limit_bytes=40 << 20),
        cost_estimate=pl.CostEstimate(flops=flops, transcendentals=0, bytes_accessed=positions << 20),
    )


def forward_call(rank, wanted, tile, probe):
    tab, prop = tables()
    return pl.pallas_call(
        lambda *refs: forward_kernel(rank, *refs),
        out_shape=(
            jax.ShapeDtypeStruct((PAIRS, 2, 2, N, N), F32),
            jax.ShapeDtypeStruct((PAIRS, 2, 2, N, N), BF16),
        ),
        in_specs=[SMEM] + [VMEM] * 4,
        out_specs=(ANY, ANY),
        scratch_shapes=[WIDE, LISTED] + PER_PAIR,
        name=f"forward_{rank}",
        **params(16, 3),
    )(wanted, tile, probe, tab, prop)


def backward_call(rank, wanted, tile, probe, ints, exits, psi, *carried):
    tab, prop = tables()
    return pl.pallas_call(
        lambda *refs: backward_kernel(rank, *refs),
        out_shape=(jax.ShapeDtypeStruct((2, 2, T, T), F32), jax.ShapeDtypeStruct((2, N, N), F32)),
        in_specs=[SMEM] + [VMEM] * 5 + [ANY, ANY] + [VMEM] * len(carried),
        out_specs=(VMEM, VMEM),
        scratch_shapes=[WIDE, WIDE, WIDE, LISTED] + PER_PAIR,
        name=f"backward_{rank}",
        **params(16, 3),
    )(wanted, tile, probe, tab, prop, ints, exits, psi, *carried)


def pack_kernel(slots, values, *outs):
    for i in range(values.shape[0]):
        slot = slots[i]
        for rank in range(CAP):

            @pl.when(slot % CAP == rank)
            def _():
                outs[rank][slot // CAP] = values[i].astype(BF16)


def pack_call(slots, intensities):
    out = jax.ShapeDtypeStruct((SOURCES, N, N), BF16)
    return pl.pallas_call(
        pack_kernel,
        out_shape=(out,) * CAP,
        in_specs=[SMEM, VMEM],
        out_specs=(VMEM,) * CAP,
        compiler_params=pltpu.CompilerParams(vmem_limit_bytes=40 << 20),
        name="pack",
    )(slots, intensities)


def extended(x, sides, width):
    for axis, dim in sides:
        size, length = (lax.axis_size(axis), x.shape[dim])
        up = [(i, (i + 1) % size) for i in range(size)]
        down = [(j, i) for i, j in up]
        last = lax.slice_in_dim(x, length - width, length, axis=dim)
        first = lax.slice_in_dim(x, 0, width, axis=dim)
        before = lax.ppermute(last, axis, up)
        after = lax.ppermute(first, axis, down)
        x = jnp.concatenate([before, x, after], axis=dim)
    return x


def tv_local(padded):
    corner_cells = padded[:, :, :-1, :-1]
    down_diff = padded[:, :, 1:, :-1] - corner_cells
    right_diff = padded[:, :, :-1, 1:] - corner_cells
    weight = 1.0 / jnp.sqrt(
        jnp.sum(down_diff * down_diff + right_diff * right_diff, axis=1, keepdims=True) + tv_smooth
    )
    flow_down = weight * down_diff
    flow_right = weight * right_diff
    return (
        flow_down[:, :, :-1, 1:]
        + flow_right[:, :, 1:, :-1]
        - flow_down[:, :, 1:, 1:]
        - flow_right[:, :, 1:, 1:]
    )


def over_all(x):
    devices = lax.axis_size(BATCH_TILE)
    shares = lax.all_to_all(
        x.reshape(devices, -1, 128), BATCH_TILE, split_axis=0, concat_axis=0, tiled=True
    )
    mine = jnp.broadcast_to(jnp.sum(shares, 0, keepdims=True), shares.shape)
    return lax.all_to_all(mine, BATCH_TILE, split_axis=0, concat_axis=0, tiled=True).reshape(x.shape)


def on_device(object_field, probe_wave, intensities, owner_rows, offsets):
    local_rows = intensities.shape[0]
    nbatch = lax.axis_size(BATCH)
    slots_all = nbatch * CAP
    targets = owner_rows[:, 0]
    serial = jnp.arange(local_rows, dtype=jnp.int32)
    earlier = (targets[:, None] == targets[None, :]) & (serial[None, :] < serial[:, None])
    slot_of = targets * CAP + jnp.sum(earlier.astype(jnp.int32), axis=1)
    hit = slot_of[:, None] == jnp.arange(slots_all, dtype=jnp.int32)[None, :]
    request = jnp.sum(jnp.where(hit[:, :, None], offsets[:, None, :] + 1, 0), axis=0)
    wanted = lax.all_to_all(
        request.reshape(nbatch, CAP * 2), BATCH, split_axis=0, concat_axis=0, tiled=True
    ).reshape(slots_all * 2)
    sent = pack_call(slot_of, intensities)
    padded = extended(object_field, ((BATCH, 2),), 1)

    def exchange(one):
        return lax.all_to_all(one, BATCH, split_axis=0, concat_axis=0, tiled=True)

    ints_0 = exchange(sent[0])
    exits_0, psi_0 = forward_call(0, wanted, object_field, probe_wave)
    later, exits_0 = lax.optimization_barrier((sent[1], exits_0))
    ints_1 = exchange(later)
    exits_1, psi_1 = forward_call(1, wanted, object_field, probe_wave)
    half = backward_call(0, wanted, object_field, probe_wave, ints_0, exits_0, psi_0)
    field_grad, probe_local = backward_call(
        1, wanted, object_field, probe_wave, ints_1, exits_1, psi_1, *half
    )
    padded, probe_local = lax.optimization_barrier((padded, probe_local))
    probe_total = over_all(probe_local)
    padded = extended(padded, ((TILE, 3),), 1)
    new_object = object_field - update_rate * (field_grad + tv_weight * tv_local(padded))
    new_probe = probe_wave.astype(F32) - probe_rate * probe_total
    return (new_object, new_probe)


def solution(mesh):
    finer = Mesh(mesh.devices.reshape(4, 4, 4, 2), ("batch_0", "batch_1", "tile_0", "tile_1"))
    placed = (P(None, None, BATCH, TILE), P(), P(BATCH_TILE), P(BATCH_TILE), P(BATCH_TILE))
    return jax.shard_map(
        on_device,
        mesh=finer,
        in_specs=placed,
        out_specs=(P(None, None, BATCH, TILE), P()),
        check_vma=False,
    )
```

time: 350 us -> 201 us (0.57)
  waiting for transfers between devices: 240 us -> 7.07 us
  starting transfers between devices: 22.9 us -> 91.1 us
  local copies, waits for them, and re-layouts: 6.24 us -> 28.5 us
  between operations: 14.1 us -> 0.9 us
  other arithmetic: 16.9 us -> 26.6 us
  Pallas kernels: 49.9 us -> 45.4 us
    psum x1 -> x0, waiting for transfers between devices: 188 us -> none  [on_device(): probe_total = lax.psum(probe_local, BATCH_TILE)]
    all_to_all x1 -> x4, starting transfers between devices: 6.81 us -> 74.9 us  [the longest x1 52.9 us: over_all(): lax.all_to_all(x.reshape(devices, -1, 128), BATCH_TILE, split_axis=0, con...]
    ppermute x2, waiting for transfers between devices: 46.5 us -> 0.01 us  [extended(): before = lax.ppermute(last, axis, up)]
    unnamed x4 -> x38, local copies, waits for them, and re-layouts: 0.01 us -> 18.1 us
    all_to_all x1 -> x4, waiting for transfers between devices: 0.01 us -> 7.06 us  [the longest x1 5 us: over_all(): lax.all_to_all(mine, BATCH_TILE, split_axis=0, concat_axis=0, tiled=True)]
    ppermute x2, waiting for transfers between devices: 6 us -> 0.01 us  [extended(): after = lax.ppermute(first, axis, down)]
    sub x2 -> x1, other arithmetic: 3.67 us -> 8.55 us  [on_device(): object_field - update_rate * (field_grad + tv_weight * tv_local(padded))]
    pallas_call x2 -> x5, Pallas kernels: 49.9 us -> 45.4 us  [the longest x2 25.2 us: backward_call(): pl.pallas_call(lambda *refs: backward_kernel(rank, *refs), out_shape=(jax...]
  transfers between devices with their start and end apart: 7 -> 9, of which waited for: 4 -> 2; matrix products, arithmetic and copies ran while one was open for 5% -> 14% of each run, Pallas kernels for 3% -> 21%
where the time goes in v1:
time: 201 us; the launch traced here: 200 us
  starting transfers between devices  91.1 us (45%)
  Pallas kernels  45.4 us (23%)
  local copies, waits for them, and re-layouts  28.5 us (14%)
  other arithmetic  26.6 us (13%)
  waiting for transfers between devices  7.07 us (4%)
    all_to_all x1, starting transfers between devices, over_all(): lax.all_to_all(x.reshape(devices, -1, 128), BATCH_TILE, split_axis=0, con...  52.9 us
    pallas_call x2, Pallas kernels, backward_call(): pl.pallas_call(lambda *refs: backward_kernel(rank, *refs), out_shape=(jax...  25.2 us
    pallas_call x2, Pallas kernels, forward_call(): pl.pallas_call(lambda *refs: forward_kernel(rank, *refs), out_shape=(jax....  19.2 us
    unnamed x38, local copies, waits for them, and re-layouts  18.1 us
    all_to_all x2, starting transfers between devices, exchange(): return lax.all_to_all(one, BATCH, split_axis=0, concat_axis=0, tiled=True)  12.3 us
    all_to_all x1, starting transfers between devices, over_all(): lax.all_to_all(mine, BATCH_TILE, split_axis=0, concat_axis=0, tiled=True)  9.76 us
    sub x1, other arithmetic, on_device(): object_field - update_rate * (field_grad + tv_weight * tv_local(padded))  8.55 us
    all_to_all x1, starting transfers between devices, on_device(): lax.all_to_all(request.reshape(nbatch, CAP * 2), BATCH, split_axis=0, con...  7.57 us
  transfers between devices with their start and end apart: 9, of which 2 were waited for; matrix products, arithmetic and copies ran while one was open for 14% of the time, Pallas kernels for 21%

profile of v1, /device:TPU:1, one launch (start us, length us, event | category | flops | bytes accessed | tf_op | source)
XLA Modules:
  0.0 199.5 jit_solution(5184871614947792446)
XLA Ops:
  3.8 7.6 %all-to-all-start = ((s32[16,1,4]{2,1,0:T(1,128)}), s32[16,1,4]{2,1,0:T(1,128)S(1)}, u32[]{:S(2)}, u32[]{:S(2)}) async-start(s32[16,1,4]{2,1,0:T(1,128)} %bitcast.3), calls=%async_computation | async-start | bytes 16384 | tf_op jit(solution)/shard_map/all_to_all | solution.py:489
  12.1 2.2 %copy-done.1 = f32[16,256,256]{2,1,0:T(8,128)S(1)} copy-done((f32[16,256,256]{2,1,0:T(8,128)S(1)}, f32[16,256,256]{2,1,0:T(8,128)}, u32[]{:S(2)}) %copy-start.1) | copy-done | bytes 4194328
  18.0 7.0 %all-to-all-start.2 = ((bf16[16,256,256]{2,1,0:T(8,128)(2,1)}), bf16[16,256,256]{2,1,0:T(8,128)(2,1)}, u32[]{:S(2)}, u32[]{:S(2)}) async-start(bf16[16,256,256]{2,1,0:T(8,128)(2,1)} %copy-done.4), calls=%async_computation.2 | async-start | bytes 4194304 | tf_op jit(solution)/shard_map/all_to_all | solution.py:496
  26.9 3.5 %collective-permute-start.1 = (f32[2,2,1,384]{3,2,1,0:T(1,128)}, f32[2,2,1,384]{3,2,1,0:T(1,128)}, u32[]{:S(2)}, u32[]{:S(2)}) collective-permute-start(f32[2,2,1,384]{3,2,1,0:T(1,128)} %get-tuple-element.35), channel_id=1, source_target_pairs={{8,0},{16,8},{24,16},{32,24},{40,32},{48,40},{56,48},{64,56},{72,6... | collective-permute-start | bytes 18440 | tf_op jit(solution)/shard_map/ppermute | solution.py:448
  31.7 18.3 %forward_0.1 = (f32[8,2,2,256,256]{4,3,2,1,0:T(8,128)}, bf16[8,2,2,256,256]{4,3,2,1,0:T(8,128)(2,1)S(1)}) custom-call(s32[64]{0:T(128)S(1)} %reshape.52.refs_0_, f32[2,2,384,384]{3,2,1,0:T(8,128)S(1)} %copy-done, bf16[2,256,256]{2,1,0:T(8,128)(2,1)S(1)} %copy-done.5, bf16[3,256,256]{2,1,0:T(8,128)(2,1)S(1)} %copy-done.8, f32[2,256,256]{2,1,0:T(8,128)S(1)} %copy-done.6), custom_call_target="tpu_custom_call" | custom-call | flops 12884901888 | bytes 16777216 | tf_op jit(solution)/shard_map/forward_0/pallas_call | solution.py:391
  50.0 2.0 %copy-done.10 = bf16[8,2,2,256,256]{4,3,2,1,0:T(8,128)(2,1)} copy-done((bf16[8,2,2,256,256]{4,3,2,1,0:T(8,128)(2,1)}, bf16[8,2,2,256,256]{4,3,2,1,0:T(8,128)(2,1)S(1)}, u32[]{:S(2)}) %copy-start.10) | copy-done | bytes 4194328
  52.0 2.1 %all-to-all-done.2.refs_5_ = bf16[16,256,256]{2,1,0:T(8,128)(2,1)} async-done(((bf16[16,256,256]{2,1,0:T(8,128)(2,1)}), bf16[16,256,256]{2,1,0:T(8,128)(2,1)}, u32[]{:S(2)}, u32[]{:S(2)}) %all-to-all-start.2) | async-done | bytes 2097184 | tf_op jit(solution)/shard_map/all_to_all | solution.py:496
  54.1 5.3 %all-to-all-start.1 = ((bf16[16,256,256]{2,1,0:T(8,128)(2,1)}), bf16[16,256,256]{2,1,0:T(8,128)(2,1)}, u32[]{:S(2)}, u32[]{:S(2)}) async-start(bf16[16,256,256]{2,1,0:T(8,128)(2,1)} %copy-done.3), calls=%async_computation.1 | async-start | bytes 4194304 | tf_op jit(solution)/shard_map/all_to_all | solution.py:496
  60.3 1.9 copy-done.9
  62.3 2.5 %pad_maximum_fusion.2 = f32[2,2,386,384]{3,2,1,0:T(8,128)} fusion(f32[2,2,1,384]{3,2,1,0:T(1,128)} %collective-permute-done.1, f32[2,2,384,384]{3,2,1,0:T(8,128)S(1)} %copy-done, f32[2,2,1,384]{3,2,1,0:T(1,128)} %collective-permute-done), kind=kLoop, calls=%fused_computation.5 | loop fusion | flops 1185792 | bytes 4743168 | tf_op jit(solution)/shard_map/concatenate | solution.py:449
  65.1 22.3 %backward_0.1 = (f32[2,2,384,384]{3,2,1,0:T(8,128)S(1)}, f32[2,256,256]{2,1,0:T(8,128)S(1)}) custom-call(s32[64]{0:T(128)S(1)} %reshape.52.refs_0_, f32[2,2,384,384]{3,2,1,0:T(8,128)S(1)} %copy-done, bf16[2,256,256]{2,1,0:T(8,128)(2,1)S(1)} %copy-done.5, bf16[3,256,256]{2,1,0:T(8,128)(2,1)S(1)} %copy-done.8, f32[2,256,256]{2,1,0:T(8,128)S(1)} %copy-done.6, ...), custom_call_target="tpu_custom_call" | custom-call | flops 12884901888 | bytes 16777216 | tf_op jit(solution)/shard_map/backward_0/pallas_call | solution.py:407
  90.7 1.7 copy-done.13
  93.4 2.8 %backward_1.1 = (f32[2,2,384,384]{3,2,1,0:T(8,128)S(1)}, f32[2,256,256]{2,1,0:T(8,128)S(1)}) custom-call(s32[64]{0:T(128)S(1)} %reshape.52.refs_0_, f32[2,2,384,384]{3,2,1,0:T(8,128)S(1)} %copy-done, bf16[2,256,256]{2,1,0:T(8,128)(2,1)S(1)} %copy-done.5, bf16[3,256,256]{2,1,0:T(8,128)(2,1)S(1)} %copy-done.8, f32[2,256,256]{2,1,0:T(8,128)S(1)} %copy-done.7, ...), custom_call_target="tpu_custom_call" | custom-call | flops 12884901888 | bytes 16777216 | tf_op jit(solution)/shard_map/backward_1/pallas_call | solution.py:407
  99.1 1.5 copy.25
  100.5 3.8 %collective-permute-start.2 = (f32[2,2,386,1]{2,1,3,0:T(2,128)S(1)}, f32[2,2,386,1]{2,1,3,0:T(2,128)S(1)}, u32[]{:S(2)}, u32[]{:S(2)}) collective-permute-start(f32[2,2,386,1]{2,1,3,0:T(2,128)S(1)} %copy.25), channel_id=1, source_target_pairs={{0,1},{1,2},{2,3},{3,4},{4,5},{5,6},{6,7},{7,0},{8,9},{9,10},{10,1... | collective-permute-start | bytes 18536 | tf_op jit(solution)/shard_map/ppermute | solution.py:447
  104.3 1.5 copy.27
  106.6 52.9 %all-to-all-start.3 = ((f32[128,8,128]{2,1,0:T(8,128)}), f32[128,8,128]{2,1,0:T(8,128)}, u32[]{:S(2)}, u32[]{:S(2)}) async-start(f32[128,8,128]{2,1,0:T(8,128)} %reshape.53), calls=%async_computation.3 | async-start | bytes 1048576 | tf_op jit(solution)/shard_map/all_to_all | solution.py:472
  159.8 1.9 copy.28
  161.7 5.8 %add_reduce_fusion = f32[2,385,385]{2,1,0:T(8,128)S(1)} fusion(f32[2,2,386,384]{3,2,1,0:T(8,128)} %pad_maximum_fusion.2, f32[2,2,386,1]{3,2,1,0:T(8,128)S(1)} %copy.26, f32[2,2,386,1]{3,2,1,0:T(8,128)} %copy.28), kind=kLoop, calls=%fused_computation.4 | loop fusion | flops 5039650 | bytes 3569736 | tf_op jit(solution)/shard_map/reduce_sum | solution.py:458
  167.8 1.4 copy-done.17
  169.4 3.7 %broadcast_multiply_fusion.1 = (f32[2,2,385,385]{3,2,1,0:T(8,128)}, f32[2,2,385,385]{3,2,1,0:T(8,128)}) fusion(f32[2,385,385]{2,1,0:T(8,128)S(1)} %add_rsqrt_fusion, f32[2,2,386,384]{3,2,1,0:T(8,128)S(1)} %copy-done.17, f32[2,2,386,1]{3,2,1,0:T(8,128)S(1)} %copy.26, f32[2,2,386,1]{3,2,1,0:T(8,128)S(1)} %copy-done.18), kind=kLoop, calls=%fused_computation.14 | loop fusion | flops 4150300 | bytes 8312936 | tf_op jit(solution)/shard_map/mul | solution.py:460
  175.1 9.8 %all-to-all-start.4 = ((f32[128,8,128]{2,1,0:T(8,128)}), f32[128,8,128]{2,1,0:T(8,128)S(1)}, u32[]{:S(2)}, u32[]{:S(2)}) async-start(f32[128,8,128]{2,1,0:T(8,128)} %broadcast_in_dim.36), calls=%async_computation.4 | async-start | bytes 1048576 | tf_op jit(solution)/shard_map/all_to_all | solution.py:476
  184.9 8.5 %fusion.5 = f32[2,2,384,384]{3,2,1,0:T(8,128)} fusion(f32[2,2,384,384]{3,2,1,0:T(8,128)S(1)} %copy-done, f32[2,2,384,384]{3,2,1,0:T(8,128)} %copy-done.2, f32[2,2,385,385]{3,2,1,0:T(8,128)} %get-tuple-element.31, f32[2,2,385,385]{3,2,1,0:T(8,128)} %get-tuple-element.30), kind=kLoop, calls=%fused_computation.10 | loop fusion | flops 4128768 | bytes 16515072 | tf_op jit(solution)/shard_map/sub | solution.py:510
  193.5 5.0 %all-to-all-done.4 = f32[128,8,128]{2,1,0:T(8,128)S(1)} async-done(((f32[128,8,128]{2,1,0:T(8,128)}), f32[128,8,128]{2,1,0:T(8,128)S(1)}, u32[]{:S(2)}, u32[]{:S(2)}) %all-to-all-start.4) | async-done | bytes 524320 | tf_op jit(solution)/shard_map/all_to_all | solution.py:476
  (65 shorter events, 23.7 us)
Async XLA Ops:
  3.8 14.2 %all-to-all-start = ((s32[16,1,4]{2,1,0:T(1,128)}), s32[16,1,4]{2,1,0:T(1,128)S(1)}, u32[]{:S(2)}, u32[]{:S(2)}) async-start(s32[16,1,4]{2,1,0:T(1,128)} %bitcast.3), calls=%async_computation | async-start | bytes 16384 | tf_op jit(solution)/shard_map/all_to_all | solution.py:489
  12.1 2.2 %copy-start.1 = (f32[16,256,256]{2,1,0:T(8,128)S(1)}, f32[16,256,256]{2,1,0:T(8,128)}, u32[]{:S(2)}) copy-start(f32[16,256,256]{2,1,0:T(8,128)} %values.1) | copy-start | bytes 12582916
  15.3 1.4 copy-start.3
  18.0 7.0 %copy-start = (f32[2,2,384,384]{3,2,1,0:T(8,128)S(1)}, f32[2,2,384,384]{3,2,1,0:T(8,128)}, u32[]{:S(2)}) copy-start(f32[2,2,384,384]{3,2,1,0:T(8,128)} %refs_1_.7) | copy-start | bytes 7077892
  18.0 13.7 %copy-start.5 = (bf16[2,256,256]{2,1,0:T(8,128)(2,1)S(1)}, bf16[2,256,256]{2,1,0:T(8,128)(2,1)}, u32[]{:S(2)}) copy-start(bf16[2,256,256]{2,1,0:T(8,128)(2,1)} %refs_2_.7) | copy-start | bytes 786436
  18.0 13.7 %copy-start.6 = (f32[2,256,256]{2,1,0:T(8,128)S(1)}, f32[2,256,256]{2,1,0:T(8,128)}, u32[]{:S(2)}) copy-start(f32[2,256,256]{2,1,0:T(8,128)} %constant.21.clone.refs_4_) | copy-start | bytes 1572868
  18.0 13.7 %copy-start.8 = (bf16[3,256,256]{2,1,0:T(8,128)(2,1)S(1)}, bf16[3,256,256]{2,1,0:T(8,128)(2,1)}, u32[]{:S(2)}) copy-start(bf16[3,256,256]{2,1,0:T(8,128)(2,1)} %constant.20.clone.refs_3_) | copy-start | bytes 1179652
  18.0 36.1 %all-to-all-start.2 = ((bf16[16,256,256]{2,1,0:T(8,128)(2,1)}), bf16[16,256,256]{2,1,0:T(8,128)(2,1)}, u32[]{:S(2)}, u32[]{:S(2)}) async-start(bf16[16,256,256]{2,1,0:T(8,128)(2,1)} %copy-done.4), calls=%async_computation.2 | async-start | bytes 4194304 | tf_op jit(solution)/shard_map/all_to_all | solution.py:496
  25.6 36.7 %collective-permute-start = (f32[2,2,1,384]{3,2,1,0:T(1,128)}, f32[2,2,1,384]{3,2,1,0:T(1,128)}, u32[]{:S(2)}, u32[]{:S(2)}) collective-permute-start(f32[2,2,1,384]{3,2,1,0:T(1,128)} %get-tuple-element.34), channel_id=1, source_target_pairs={{0,8},{8,16},{16,24},{24,32},{32,40},{40,48},{48,56},{56,64},{64,7... | collective-permute-start | bytes 18440 | tf_op jit(solution)/shard_map/ppermute | solution.py:447
  26.9 35.4 %collective-permute-start.1 = (f32[2,2,1,384]{3,2,1,0:T(1,128)}, f32[2,2,1,384]{3,2,1,0:T(1,128)}, u32[]{:S(2)}, u32[]{:S(2)}) collective-permute-start(f32[2,2,1,384]{3,2,1,0:T(1,128)} %get-tuple-element.35), channel_id=1, source_target_pairs={{8,0},{16,8},{24,16},{32,24},{40,32},{48,40},{56,48},{64,56},{72,6... | collective-permute-start | bytes 18440 | tf_op jit(solution)/shard_map/ppermute | solution.py:448
  50.0 2.0 %copy-start.10 = (bf16[8,2,2,256,256]{4,3,2,1,0:T(8,128)(2,1)}, bf16[8,2,2,256,256]{4,3,2,1,0:T(8,128)(2,1)S(1)}, u32[]{:S(2)}) copy-start(bf16[8,2,2,256,256]{4,3,2,1,0:T(8,128)(2,1)S(1)} %get-tuple-element.23.refs_7_) | copy-start | bytes 12582916
  54.1 35.6 %all-to-all-start.1 = ((bf16[16,256,256]{2,1,0:T(8,128)(2,1)}), bf16[16,256,256]{2,1,0:T(8,128)(2,1)}, u32[]{:S(2)}, u32[]{:S(2)}) async-start(bf16[16,256,256]{2,1,0:T(8,128)(2,1)} %copy-done.3), calls=%async_computation.1 | async-start | bytes 4194304 | tf_op jit(solution)/shard_map/all_to_all | solution.py:496
  60.3 1.9 copy-start.9
  62.3 2.8 %copy-start.11 = (bf16[8,2,2,256,256]{4,3,2,1,0:T(8,128)(2,1)S(1)}, bf16[8,2,2,256,256]{4,3,2,1,0:T(8,128)(2,1)}, u32[]{:S(2)}) copy-start(bf16[8,2,2,256,256]{4,3,2,1,0:T(8,128)(2,1)} %copy-done.10) | copy-start | bytes 12582916
  87.4 1.4 copy-start.12
  90.7 1.7 copy-start.13
  93.4 4.2 %copy-start.16 = (f32[2,2,386,384]{3,2,1,0:T(8,128)S(1)}, f32[2,2,386,384]{3,2,1,0:T(8,128)}, u32[]{:S(2)}) copy-start(f32[2,2,386,384]{3,2,1,0:T(8,128)} %pad_maximum_fusion.2) | copy-start | bytes 7114756
  96.2 1.4 copy-start.2
  100.5 59.0 %collective-permute-start.2 = (f32[2,2,386,1]{2,1,3,0:T(2,128)S(1)}, f32[2,2,386,1]{2,1,3,0:T(2,128)S(1)}, u32[]{:S(2)}, u32[]{:S(2)}) collective-permute-start(f32[2,2,386,1]{2,1,3,0:T(2,128)S(1)} %copy.25), channel_id=1, source_target_pairs={{0,1},{1,2},{2,3},{3,4},{4,5},{5,6},{6,7},{7,0},{8,9},{9,10},{10,1... | collective-permute-start | bytes 18536 | tf_op jit(solution)/shard_map/ppermute | solution.py:447
  105.7 54.1 %collective-permute-start.3 = (f32[2,2,386,1]{2,1,3,0:T(2,128)S(1)}, f32[2,2,386,1]{2,1,3,0:T(2,128)}, u32[]{:S(2)}, u32[]{:S(2)}) collective-permute-start(f32[2,2,386,1]{2,1,3,0:T(2,128)S(1)} %copy.27), channel_id=1, source_target_pairs={{1,0},{2,1},{3,2},{4,3},{5,4},{6,5},{7,6},{0,7},{9,8},{10,9},{11,1... | collective-permute-start | bytes 18536 | tf_op jit(solution)/shard_map/ppermute | solution.py:448
  106.6 66.6 %all-to-all-start.3 = ((f32[128,8,128]{2,1,0:T(8,128)}), f32[128,8,128]{2,1,0:T(8,128)}, u32[]{:S(2)}, u32[]{:S(2)}) async-start(f32[128,8,128]{2,1,0:T(8,128)} %reshape.53), calls=%async_computation.3 | async-start | bytes 1048576 | tf_op jit(solution)/shard_map/all_to_all | solution.py:472
  167.6 1.7 copy-start.17
  167.6 1.9 copy-start.18
  175.1 23.3 %all-to-all-start.4 = ((f32[128,8,128]{2,1,0:T(8,128)}), f32[128,8,128]{2,1,0:T(8,128)S(1)}, u32[]{:S(2)}, u32[]{:S(2)}) async-start(f32[128,8,128]{2,1,0:T(8,128)} %broadcast_in_dim.36), calls=%async_computation.4 | async-start | bytes 1048576 | tf_op jit(solution)/shard_map/all_to_all | solution.py:476
  (4 other events, 4.2 us)

commit v2 on v1

--- a/solution.py
+++ b/solution.py
@@ -209,19 +209,18 @@
                 live.remove(one)
 
 
-def list_used(wanted, listed, rank):
+def list_used(wanted, listed):
     def one(k, used):
         listed[used] = k
-        return used + (wanted[2 * CAP * k + 2 * rank] > 0).astype(jnp.int32)
-
-    return lax.fori_loop(0, SOURCES, one, jnp.int32(0))
-
-
-def chosen(wanted, listed, count, pair, rank):
+        return used + (wanted[2 * k] > 0).astype(jnp.int32)
+
+    return lax.fori_loop(0, SLOTS, one, jnp.int32(0))
+
+
+def chosen(wanted, listed, count, pair):
     there = 2 * pair + 1 < count
     slots = listed[2 * pair], listed[jnp.where(there, 2 * pair + 1, 2 * pair)]
-    at = [2 * CAP * k + 2 * rank for k in slots]
-    return slots, [(wanted[a] - 1, wanted[a + 1] - 1) for a in at], there
+    return slots, [(wanted[2 * k] - 1, wanted[2 * k + 1] - 1) for k in slots], there
 
 
 def round_tile(tile_in, tile):
@@ -242,9 +241,20 @@
     pl.run_scoped(start, refs, refs)
 
 
-def forward_kernel(rank, wanted, tile_in, probe, tab, prop, exits_out, psi_out, tile, listed, x, y, exits, psi, sems):
+def forward_kernel(
+    wanted, tile_in, probe, tab, prop, exits_out, psi_out, edge_rows, edge_cols, tile, listed, x, y, exits, psi, sems
+):
     round_tile(tile_in, tile)
+    for s in range(2):
+        for q in range(2):
+            k = 2 * s + q
+            edge_rows[k : k + 1] = tile_in[s, q, 0:1, :]
+            edge_rows[4 + k : 5 + k] = tile_in[s, q, T - 1 : T, :]
+            edge_cols[k : k + 1] = jnp.transpose(tile_in[s, q, :, 0:128])[0:1]
+            edge_cols[4 + k : 5 + k] = jnp.transpose(tile_in[s, q, :, T - 128 : T])[127:128]
     env = (tile, probe, tab, prop)
+    count = list_used(wanted, listed)
+    pairs = (count + 1) // 2
 
     def copies(b, at):
         return (
@@ -252,14 +262,11 @@
             pltpu.make_async_copy(psi.at[b], psi_out.at[at], sems.at[1, b]),
         )
 
-    count = list_used(wanted, listed, rank)
-    pairs = (count + 1) // 2
-
     def body(acc_a, acc_b):
         @pl.loop(0, pairs)
         def _(pair):
             b = pair % 2
-            _, at, _ = chosen(wanted, listed, count, pair, rank)
+            _, at, _ = chosen(wanted, listed, count, pair)
 
             @pl.when(pair >= 2)
             def _():
@@ -293,13 +300,11 @@
     with_accumulators(body)
 
 
-def backward_kernel(rank, *refs):
-    wanted, tile_in, probe, tab, prop, ints, exits_in, psi_in = refs[:8]
-    refs = refs[8:]
-    if rank:
-        (field_in, probe_in), refs = refs[:2], refs[2:]
-    field_out, probe_sum, tile, field_a, field_b, listed, x, y, exits, psi, sems = refs
-    count = list_used(wanted, listed, rank)
+def backward_kernel(
+    wanted, tile_in, probe, tab, prop, ints, exits_in, psi_in, field_out, probe_sum, *scratch
+):
+    tile, field_a, field_b, listed, x, y, exits, psi, sems = scratch
+    count = list_used(wanted, listed)
     pairs = (count + 1) // 2
 
     def copies(b, at):
@@ -314,20 +319,19 @@
             one.start()
 
     round_tile(tile_in, tile)
-    for s in range(2):
-        for q in range(2):
-            for k in range(3):
-                at = pl.ds(128 * k, 128)
-                field_a[s, q, k] = field_in[s, q, :, at] if rank else jnp.zeros((T, 128), F32)
-                field_b[s, q, k] = jnp.zeros((T, 128), F32)
-    probe_sum[...] = probe_in[...] if rank else jnp.zeros((2, N, N), F32)
+    for field in (field_a, field_b):
+        for s in range(2):
+            for q in range(2):
+                for k in range(3):
+                    field[s, q, k] = jnp.zeros((T, 128), F32)
+    probe_sum[...] = jnp.zeros((2, N, N), F32)
     env = (tile, probe, tab, prop, probe_sum)
 
     def body(acc_a, acc_b):
         @pl.loop(0, pairs)
         def _(pair):
             b = pair % 2
-            slots, at, there = chosen(wanted, listed, count, pair, rank)
+            slots, at, there = chosen(wanted, listed, count, pair)
 
             @pl.when(pair + 1 < pairs)
             def _():
@@ -362,118 +366,152 @@
                 field_out[s, q, :, pl.ds(128 * k, 128)] = field_a[s, q, k] + field_b[s, q, k]
 
 
+def finish_kernel(tile, field, edge_rows, edge_cols, out, padded, flat):
+    flat[...] = jnp.zeros((128, 512), F32)
+    flat[0:8] = edge_cols[...]
+    tall = jnp.transpose(flat[...])
+    for s in range(2):
+        for q in range(2):
+            k = 2 * s + q
+            padded[s, q, 8 : 8 + T, 128 : 128 + T] = tile[s, q]
+            padded[s, q, 7:8, 128 : 128 + T] = edge_rows[k : k + 1]
+            padded[s, q, 8 + T : 9 + T, 128 : 128 + T] = edge_rows[4 + k : 5 + k]
+            after, before = tall[:, k : k + 1], tall[:, 4 + k : 5 + k]
+            padded[s, q, 8 : 8 + T, 128 + T : 256 + T] = jnp.broadcast_to(after[:T], (T, 128))
+            padded[s, q, 8 : 8 + T, 0:128] = jnp.broadcast_to(before[:T], (T, 128))
+            padded[s, q, 7:8, 128 + T : 256 + T] = jnp.broadcast_to(after[T : T + 1], (1, 128))
+            padded[s, q, 8 + T : 9 + T, 0:128] = jnp.broadcast_to(before[T : T + 1], (1, 128))
+    for s in range(2):
+
+        def part(at, down, right):
+            here = [padded[s, q, at + 8 + down : at + 8 + down + 16, 128 + right : 128 + right + T] for q in range(2)]
+            return here
+
+        for at in range(0, T, 16):
+            here, below, right = part(at, 0, 0), part(at, 1, 0), part(at, 0, 1)
+            above, above_right = part(at, -1, 0), part(at, -1, 1)
+            left, left_below = part(at, 0, -1), part(at, 1, -1)
+
+            def slopes(one, lower, righter):
+                dy = [b - a for a, b in zip(one, lower)]
+                dx = [b - a for a, b in zip(one, righter)]
+                total = dy[0] * dy[0] + dx[0] * dx[0] + (dy[1] * dy[1] + dx[1] * dx[1])
+                return dy, dx, 1.0 / jnp.sqrt(total + tv_smooth)
+
+            dy, dx, m = slopes(here, below, right)
+            dy_up, _, m_up = slopes(above, here, above_right)
+            _, dx_left, m_left = slopes(left, left_below, here)
+            for q in range(2):
+                tv = m_up * dy_up[q] + m_left * dx_left[q] - m * dy[q] - m * dx[q]
+                grad = field[s, q, at : at + 16] + tv_weight * tv
+                out[s, q, at : at + 16] = here[q] - update_rate * grad
+
+
 VMEM = pl.BlockSpec(memory_space=pltpu.VMEM)
 SMEM = pl.BlockSpec(memory_space=pltpu.SMEM)
-ANY = pl.BlockSpec(memory_space=pl.ANY)
+HBM = pl.BlockSpec(memory_space=pltpu.HBM)
 SOURCES = 16
-PAIRS = SOURCES // 2
+SLOTS = SOURCES * CAP
+PAIRS = SLOTS // 2
 WIDE = pltpu.VMEM((2, 2, 3, T, 128), F32)
-PER_PAIR = [
-    pltpu.VMEM((2, 2, N, N), BF16),
-    pltpu.VMEM((2, 2, N, N), BF16),
+TWO = pltpu.VMEM((2, 2, N, N), BF16)
+FRONTS = [
     pltpu.VMEM((2, 2, 2, N, N), F32),
     pltpu.VMEM((2, 2, 2, N, N), BF16),
     pltpu.SemaphoreType.DMA((2, 2)),
 ]
-LISTED = pltpu.SMEM((SOURCES + 1,), jnp.int32)
-
-
-def params(positions, steps):
-    flops = positions * steps * 2 * 8 * N**3
+LISTED = pltpu.SMEM((SLOTS + 1,), jnp.int32)
+
+
+def params(limit):
+    flops = SLOTS * 3 * 2 * 8 * N**3
     return dict(
-        compiler_params=pltpu.CompilerParams(vmem_limit_bytes=40 << 20),
-        cost_estimate=pl.CostEstimate(flops=flops, transcendentals=0, bytes_accessed=positions << 20),
+        compiler_params=pltpu.CompilerParams(vmem_limit_bytes=limit << 20),
+        cost_estimate=pl.CostEstimate(flops=flops, transcendentals=0, bytes_accessed=32 << 20),
     )
 
 
-def forward_call(rank, wanted, tile, probe):
+def forward_call(wanted, tile, probe):
     tab, prop = tables()
     return pl.pallas_call(
-        lambda *refs: forward_kernel(rank, *refs),
+        forward_kernel,
         out_shape=(
             jax.ShapeDtypeStruct((PAIRS, 2, 2, N, N), F32),
             jax.ShapeDtypeStruct((PAIRS, 2, 2, N, N), BF16),
+            jax.ShapeDtypeStruct((8, T), F32),
+            jax.ShapeDtypeStruct((8, T), F32),
         ),
         in_specs=[SMEM] + [VMEM] * 4,
-        out_specs=(ANY, ANY),
-        scratch_shapes=[WIDE, LISTED] + PER_PAIR,
-        name=f"forward_{rank}",
-        **params(16, 3),
+        out_specs=(HBM, HBM, VMEM, VMEM),
+        scratch_shapes=[WIDE, LISTED, TWO, TWO] + FRONTS,
+        name="forward",
+        **params(57),
     )(wanted, tile, probe, tab, prop)
 
 
-def backward_call(rank, wanted, tile, probe, ints, exits, psi, *carried):
+def backward_call(wanted, tile, probe, ints, exits, psi):
     tab, prop = tables()
     return pl.pallas_call(
-        lambda *refs: backward_kernel(rank, *refs),
+        backward_kernel,
         out_shape=(jax.ShapeDtypeStruct((2, 2, T, T), F32), jax.ShapeDtypeStruct((2, N, N), F32)),
-        in_specs=[SMEM] + [VMEM] * 5 + [ANY, ANY] + [VMEM] * len(carried),
+        in_specs=[SMEM] + [VMEM] * 5 + [HBM, HBM],
         out_specs=(VMEM, VMEM),
-        scratch_shapes=[WIDE, WIDE, WIDE, LISTED] + PER_PAIR,
-        name=f"backward_{rank}",
-        **params(16, 3),
-    )(wanted, tile, probe, tab, prop, ints, exits, psi, *carried)
-
-
-def pack_kernel(slots, values, *outs):
-    for i in range(values.shape[0]):
-        slot = slots[i]
-        for rank in range(CAP):
-
-            @pl.when(slot % CAP == rank)
-            def _():
-                outs[rank][slot // CAP] = values[i].astype(BF16)
+        scratch_shapes=[WIDE, WIDE, WIDE, LISTED, TWO, TWO] + FRONTS,
+        name="backward",
+        **params(57),
+    )(wanted, tile, probe, tab, prop, ints, exits, psi)
+
+
+def finish_call(tile, field, edge_rows, edge_cols):
+    return pl.pallas_call(
+        finish_kernel,
+        out_shape=jax.ShapeDtypeStruct((2, 2, T, T), F32),
+        in_specs=[VMEM] * 4,
+        out_specs=VMEM,
+        scratch_shapes=[pltpu.VMEM((2, 2, T + 16, T + 256), F32), pltpu.VMEM((128, 512), F32)],
+        compiler_params=pltpu.CompilerParams(vmem_limit_bytes=24 << 20),
+        name="finish",
+    )(tile, field, edge_rows, edge_cols)
+
+
+def pack_kernel(slots, values, out):
+    for i in range(SOURCES):
+        out[slots[i]] = values[i].astype(BF16)
 
 
 def pack_call(slots, intensities):
-    out = jax.ShapeDtypeStruct((SOURCES, N, N), BF16)
     return pl.pallas_call(
         pack_kernel,
-        out_shape=(out,) * CAP,
+        out_shape=jax.ShapeDtypeStruct((SLOTS, N, N), BF16),
         in_specs=[SMEM, VMEM],
-        out_specs=(VMEM,) * CAP,
-        compiler_params=pltpu.CompilerParams(vmem_limit_bytes=40 << 20),
+        out_specs=VMEM,
+        compiler_params=pltpu.CompilerParams(vmem_limit_bytes=24 << 20),
         name="pack",
     )(slots, intensities)
 
 
-def extended(x, sides, width):
-    for axis, dim in sides:
-        size, length = (lax.axis_size(axis), x.shape[dim])
-        up = [(i, (i + 1) % size) for i in range(size)]
-        down = [(j, i) for i, j in up]
-        last = lax.slice_in_dim(x, length - width, length, axis=dim)
-        first = lax.slice_in_dim(x, 0, width, axis=dim)
-        before = lax.ppermute(last, axis, up)
-        after = lax.ppermute(first, axis, down)
-        x = jnp.concatenate([before, x, after], axis=dim)
-    return x
-
-
-def tv_local(padded):
-    corner_cells = padded[:, :, :-1, :-1]
-    down_diff = padded[:, :, 1:, :-1] - corner_cells
-    right_diff = padded[:, :, :-1, 1:] - corner_cells
-    weight = 1.0 / jnp.sqrt(
-        jnp.sum(down_diff * down_diff + right_diff * right_diff, axis=1, keepdims=True) + tv_smooth
-    )
-    flow_down = weight * down_diff
-    flow_right = weight * right_diff
-    return (
-        flow_down[:, :, :-1, 1:]
-        + flow_right[:, :, 1:, :-1]
-        - flow_down[:, :, 1:, 1:]
-        - flow_right[:, :, 1:, 1:]
-    )
+def moved(x, axis, step):
+    size = lax.axis_size(axis)
+    return lax.ppermute(x, axis, [(i, (i + step) % size) for i in range(size)])
+
+
+def neighbours(edge_rows, edge_cols):
+    above, below = moved(edge_rows[4:], BATCH, 1), moved(edge_rows[:4], BATCH, -1)
+    for_left = jnp.concatenate([edge_cols[:4], jnp.broadcast_to(above[:, :1], (4, 128))], 1)
+    for_right = jnp.concatenate([edge_cols[4:], jnp.broadcast_to(below[:, -1:], (4, 128))], 1)
+    right, left = moved(for_left, TILE, -1), moved(for_right, TILE, 1)
+    return jnp.concatenate([above, below]), jnp.concatenate([right, left])
 
 
 def over_all(x):
     devices = lax.axis_size(BATCH_TILE)
     shares = lax.all_to_all(
-        x.reshape(devices, -1, 128), BATCH_TILE, split_axis=0, concat_axis=0, tiled=True
+        x.astype(BF16).reshape(devices, -1, 128), BATCH_TILE, split_axis=0, concat_axis=0, tiled=True
     )
-    mine = jnp.broadcast_to(jnp.sum(shares, 0, keepdims=True), shares.shape)
-    return lax.all_to_all(mine, BATCH_TILE, split_axis=0, concat_axis=0, tiled=True).reshape(x.shape)
+    mine = jnp.sum(shares.astype(F32), 0, keepdims=True).astype(BF16)
+    mine = jnp.broadcast_to(mine, shares.shape)
+    total = lax.all_to_all(mine, BATCH_TILE, split_axis=0, concat_axis=0, tiled=True)
+    return total.astype(F32).reshape(x.shape)
 
 
 def on_device(object_field, probe_wave, intensities, owner_rows, offsets):
@@ -489,25 +527,14 @@
     wanted = lax.all_to_all(
         request.reshape(nbatch, CAP * 2), BATCH, split_axis=0, concat_axis=0, tiled=True
     ).reshape(slots_all * 2)
-    sent = pack_call(slot_of, intensities)
-    padded = extended(object_field, ((BATCH, 2),), 1)
-
-    def exchange(one):
-        return lax.all_to_all(one, BATCH, split_axis=0, concat_axis=0, tiled=True)
-
-    ints_0 = exchange(sent[0])
-    exits_0, psi_0 = forward_call(0, wanted, object_field, probe_wave)
-    later, exits_0 = lax.optimization_barrier((sent[1], exits_0))
-    ints_1 = exchange(later)
-    exits_1, psi_1 = forward_call(1, wanted, object_field, probe_wave)
-    half = backward_call(0, wanted, object_field, probe_wave, ints_0, exits_0, psi_0)
-    field_grad, probe_local = backward_call(
-        1, wanted, object_field, probe_wave, ints_1, exits_1, psi_1, *half
-    )
-    padded, probe_local = lax.optimization_barrier((padded, probe_local))
+    sent = pack_call(slot_of, intensities).reshape(nbatch, CAP, N, N)
+    ints = lax.all_to_all(sent, BATCH, split_axis=0, concat_axis=0, tiled=True)
+    ints = ints.reshape(slots_all, N, N)
+    exits, psi, edge_rows, edge_cols = forward_call(wanted, object_field, probe_wave)
+    around = neighbours(edge_rows, edge_cols)
+    field_grad, probe_local = backward_call(wanted, object_field, probe_wave, ints, exits, psi)
     probe_total = over_all(probe_local)
-    padded = extended(padded, ((TILE, 3),), 1)
-    new_object = object_field - update_rate * (field_grad + tv_weight * tv_local(padded))
+    new_object = finish_call(object_field, field_grad, *around)
     new_probe = probe_wave.astype(F32) - probe_rate * probe_total
     return (new_object, new_probe)
 

time: 201 us -> 190 us (0.945)
  Pallas kernels: 45.4 us -> 70.7 us
  other arithmetic: 26.6 us -> 6.03 us
  waiting for transfers between devices: 7.07 us -> 26.8 us
  starting transfers between devices: 91.1 us -> 72 us
  local copies, waits for them, and re-layouts: 28.5 us -> 11.4 us
    all_to_all x3 -> x2, starting transfers between devices: 65.2 us -> 34.8 us  [the longest x1 28.9 us: over_all(): lax.all_to_all(x.astype(BF16).reshape(devices, -1, 128), BATCH_TILE, spli...]
    pallas_call x5 -> x4, Pallas kernels: 45.4 us -> 70.7 us  [the longest x1 25.6 us: backward_call(): pl.pallas_call(backward_kernel, out_shape=(jax.ShapeDtypeStruct((2, 2, T,...]
    all_to_all x3 -> x2, waiting for transfers between devices: 2.06 us -> 23.7 us  [the longest x1 15 us: on_device(): ints = lax.all_to_all(sent, BATCH, split_axis=0, concat_axis=0, tiled=True)]
    ppermute x4, starting transfers between devices: 8.55 us -> 24.9 us  [moved(): return lax.ppermute(x, axis, [(i, (i + step) % size) for i in range(size)])]
    unnamed x38 -> x10, local copies, waits for them, and re-layouts: 18.1 us -> 5.8 us
    sub x1 -> x0, other arithmetic: 8.55 us -> none  [on_device(): object_field - update_rate * (field_grad + tv_weight * tv_local(padded))]
    reduce_sum x2 -> x1, other arithmetic: 7.01 us -> 0.14 us  [over_all(): mine = jnp.sum(shares.astype(F32), 0, keepdims=True).astype(BF16)]
    all_to_all x1, starting transfers between devices: 9.76 us -> 4.68 us  [over_all(): lax.all_to_all(mine, BATCH_TILE, split_axis=0, concat_axis=0, tiled=True)]
  transfers between devices with their start and end apart: 9 -> 8, of which waited for: 2 -> 4; matrix products, arithmetic and copies ran while one was open for 14% -> 4% of each run, Pallas kernels for 21% -> 38%
where the time goes in v2:
time: 190 us; the launch traced here: 188 us
  starting transfers between devices  72 us (38%)
  Pallas kernels  70.7 us (37%)
  waiting for transfers between devices  26.8 us (14%)
  local copies, waits for them, and re-layouts  11.4 us (6%)
  other arithmetic  6.03 us (3%)
    all_to_all x1, starting transfers between devices, over_all(): lax.all_to_all(x.astype(BF16).reshape(devices, -1, 128), BATCH_TILE, spli...  28.9 us
    pallas_call x1, Pallas kernels, backward_call(): pl.pallas_call(backward_kernel, out_shape=(jax.ShapeDtypeStruct((2, 2, T,...  25.6 us
    ppermute x4, starting transfers between devices, moved(): return lax.ppermute(x, axis, [(i, (i + step) % size) for i in range(size)])  24.9 us
    pallas_call x1, Pallas kernels, finish_call(): pl.pallas_call(finish_kernel, out_shape=jax.ShapeDtypeStruct((2, 2, T, T)...  23.7 us
    pallas_call x1, Pallas kernels, forward_call(): pl.pallas_call(forward_kernel, out_shape=(jax.ShapeDtypeStruct((PAIRS, 2,...  20.8 us
    all_to_all x1, waiting for transfers between devices, on_device(): ints = lax.all_to_all(sent, BATCH, split_axis=0, concat_axis=0, tiled=True)  15 us
    all_to_all x1, waiting for transfers between devices, over_all(): lax.all_to_all(x.astype(BF16).reshape(devices, -1, 128), BATCH_TILE, spli...  8.74 us
    all_to_all x1, starting transfers between devices, on_device(): lax.all_to_all(request.reshape(nbatch, CAP * 2), BATCH, split_axis=0, con...  7.57 us
  transfers between devices with their start and end apart: 8, of which 4 were waited for; matrix products, arithmetic and copies ran while one was open for 4% of the time, Pallas kernels for 38%

profile of v2, /device:TPU:1, one launch (start us, length us, event | category | flops | bytes accessed | tf_op | source)
XLA Modules:
  0.0 187.7 jit_solution(13119942885766116635)
XLA Ops:
  0.6 0.9 convert_reduce_fusion
  3.8 7.6 %all-to-all-start = ((s32[16,1,4]{2,1,0:T(1,128)}), s32[16,1,4]{2,1,0:T(1,128)S(1)}, u32[]{:S(2)}, u32[]{:S(2)}) async-start(s32[16,1,4]{2,1,0:T(1,128)} %bitcast.3), calls=%async_computation | async-start | bytes 16384 | tf_op jit(solution)/shard_map/all_to_all | solution.py:527
  12.1 2.2 %copy-done.1 = f32[16,256,256]{2,1,0:T(8,128)S(1)} copy-done((f32[16,256,256]{2,1,0:T(8,128)S(1)}, f32[16,256,256]{2,1,0:T(8,128)}, u32[]{:S(2)}) %copy-start.1) | copy-done | bytes 4194328
  14.2 0.7 pack.1
  15.0 1.9 %copy-done = bf16[32,256,256]{2,1,0:T(8,128)(2,1)} copy-done((bf16[32,256,256]{2,1,0:T(8,128)(2,1)}, bf16[32,256,256]{2,1,0:T(8,128)(2,1)S(1)}, u32[]{:S(2)}) %copy-start) | copy-done | bytes 4194328
  16.9 0.8 all-to-all-done
  17.8 5.9 %all-to-all-start.1 = ((bf16[16,2,256,256]{3,2,1,0:T(8,128)(2,1)}), bf16[16,2,256,256]{3,2,1,0:T(8,128)(2,1)}, u32[]{:S(2)}, u32[]{:S(2)}) async-start(bf16[16,2,256,256]{3,2,1,0:T(8,128)(2,1)} %bitcast.11), calls=%async_computation.1 | async-start | bytes 8388608 | tf_op jit(solution)/shard_map/all_to_all | solution.py:531
  25.4 20.8 %forward.1 = (f32[16,2,2,256,256]{4,3,2,1,0:T(8,128)}, bf16[16,2,2,256,256]{4,3,2,1,0:T(8,128)(2,1)}, f32[8,384]{1,0:T(8,128)}, f32[8,384]{1,0:T(8,128)}) custom-call(s32[64]{0:T(128)} %reshape.54.wanted, f32[2,2,384,384]{3,2,1,0:T(8,128)} %tile.1, bf16[2,256,256]{2,1,0:T(8,128)(2,1)} %probe.3, bf16[3,256,256]{2,1,0:T(8,128)(2,1)} %constant.15.clone.tab, ...), custom_call_target="tpu_custom_call" | custom-call | flops 25769803776 | bytes 33554432 | tf_op jit(solution)/shard_map/forward/pallas_call | solution.py:436
  46.2 0.8 fusion.3
  47.0 21.9 %collective-permute-start = (f32[4,384]{1,0:T(4,128)S(1)}, f32[4,384]{1,0:T(4,128)S(1)}, u32[]{:S(2)}, u32[]{:S(2)}) collective-permute-start(f32[4,384]{1,0:T(4,128)S(1)} %get-tuple-element.16), channel_id=1, source_target_pairs={{0,8},{8,16},{16,24},{24,32},{32,40},{40,48},{48,56},{56,64},{64,7... | collective-permute-start | bytes 18440 | tf_op jit(solution)/shard_map/ppermute | solution.py:495
  68.9 0.8 fusion.2
  69.7 15.0 %all-to-all-done.1 = bf16[16,2,256,256]{3,2,1,0:T(8,128)(2,1)} async-done(((bf16[16,2,256,256]{3,2,1,0:T(8,128)(2,1)}), bf16[16,2,256,256]{3,2,1,0:T(8,128)(2,1)}, u32[]{:S(2)}, u32[]{:S(2)}) %all-to-all-start.1) | async-done | bytes 4194336 | tf_op jit(solution)/shard_map/all_to_all | solution.py:531
  84.7 25.6 %backward.1 = (f32[2,2,384,384]{3,2,1,0:T(8,128)}, f32[2,256,256]{2,1,0:T(8,128)}) custom-call(s32[64]{0:T(128)} %reshape.54.wanted, f32[2,2,384,384]{3,2,1,0:T(8,128)} %tile.1, bf16[2,256,256]{2,1,0:T(8,128)(2,1)} %probe.3, bf16[3,256,256]{2,1,0:T(8,128)(2,1)} %constant.15.clone.tab, f32[2,256,256]{2,1,0:T(8,128)} %constant.16.clone.prop, ...), custom_call_target="tpu_custom_call" | custom-call | flops 25769803776 | bytes 33554432 | tf_op jit(solution)/shard_map/backward/pallas_call | solution.py:454
  110.3 1.2 convert_element_type.21
  111.5 0.8 reshape.57
  112.3 28.9 %all-to-all-start.2 = ((bf16[128,8,128]{2,1,0:T(8,128)(2,1)}), bf16[128,8,128]{2,1,0:T(8,128)(2,1)S(1)}, u32[]{:S(2)}, u32[]{:S(2)}) async-start(bf16[128,8,128]{2,1,0:T(8,128)(2,1)} %reshape.57), calls=%async_computation.2 | async-start | bytes 524288 | tf_op jit(solution)/shard_map/all_to_all | solution.py:508
  141.5 1.8 collective-permute-start.3
  143.4 8.7 %all-to-all-done.2 = bf16[128,8,128]{2,1,0:T(8,128)(2,1)S(1)} async-done(((bf16[128,8,128]{2,1,0:T(8,128)(2,1)}), bf16[128,8,128]{2,1,0:T(8,128)(2,1)S(1)}, u32[]{:S(2)}, u32[]{:S(2)}) %all-to-all-start.2) | async-done | bytes 262176 | tf_op jit(solution)/shard_map/all_to_all | solution.py:508
  153.0 4.7 %all-to-all-start.3 = ((bf16[128,8,128]{2,1,0:T(8,128)(2,1)}), bf16[128,8,128]{2,1,0:T(8,128)(2,1)S(1)}, u32[]{:S(2)}, u32[]{:S(2)}) async-start(bf16[128,8,128]{2,1,0:T(8,128)(2,1)} %broadcast_in_dim.53), calls=%async_computation.3 | async-start | bytes 524288 | tf_op jit(solution)/shard_map/all_to_all | solution.py:513
  157.8 1.2 collective-permute-start.2
  159.0 2.3 %collective-permute-done.2 = f32[4,512]{1,0:T(4,128)S(1)} collective-permute-done((f32[4,512]{1,0:T(4,128)S(1)}, f32[4,512]{1,0:T(4,128)S(1)}, u32[]{:S(2)}, u32[]{:S(2)}) %collective-permute-start.2) | collective-permute-done | bytes 8224 | tf_op jit(solution)/shard_map/ppermute | solution.py:495
  161.3 1.7 copy-done.3
  163.0 23.7 %finish.1 = f32[2,2,384,384]{3,2,1,0:T(8,128)} custom-call(f32[2,2,384,384]{3,2,1,0:T(8,128)S(1)} %copy-done.2, f32[2,2,384,384]{3,2,1,0:T(8,128)S(1)} %copy-done.3, f32[8,384]{1,0:T(8,128)S(1)} %pad_maximum_fusion.1.edge_rows, f32[8,512]{1,0:T(8,128)S(1)} %pad_maximum_fusion.edge_cols), custom_call_target="tpu_custom_call" | custom-call | tf_op jit(solution)/shard_map/finish/pallas_call | solution.py:466
  186.9 0.8 convert_subtract_fusion
  (34 shorter events, 6.3 us)
Async XLA Ops:
  3.8 13.9 %all-to-all-start = ((s32[16,1,4]{2,1,0:T(1,128)}), s32[16,1,4]{2,1,0:T(1,128)S(1)}, u32[]{:S(2)}, u32[]{:S(2)}) async-start(s32[16,1,4]{2,1,0:T(1,128)} %bitcast.3), calls=%async_computation | async-start | bytes 16384 | tf_op jit(solution)/shard_map/all_to_all | solution.py:527
  12.1 2.2 %copy-start.1 = (f32[16,256,256]{2,1,0:T(8,128)S(1)}, f32[16,256,256]{2,1,0:T(8,128)}, u32[]{:S(2)}) copy-start(f32[16,256,256]{2,1,0:T(8,128)} %values.1) | copy-start | bytes 12582916
  15.0 1.9 %copy-start = (bf16[32,256,256]{2,1,0:T(8,128)(2,1)}, bf16[32,256,256]{2,1,0:T(8,128)(2,1)S(1)}, u32[]{:S(2)}) copy-start(bf16[32,256,256]{2,1,0:T(8,128)(2,1)S(1)} %pack.1) | copy-start | bytes 12582916
  17.8 66.9 %all-to-all-start.1 = ((bf16[16,2,256,256]{3,2,1,0:T(8,128)(2,1)}), bf16[16,2,256,256]{3,2,1,0:T(8,128)(2,1)}, u32[]{:S(2)}, u32[]{:S(2)}) async-start(bf16[16,2,256,256]{3,2,1,0:T(8,128)(2,1)} %bitcast.11), calls=%async_computation.1 | async-start | bytes 8388608 | tf_op jit(solution)/shard_map/all_to_all | solution.py:531
  47.0 96.3 %collective-permute-start = (f32[4,384]{1,0:T(4,128)S(1)}, f32[4,384]{1,0:T(4,128)S(1)}, u32[]{:S(2)}, u32[]{:S(2)}) collective-permute-start(f32[4,384]{1,0:T(4,128)S(1)} %get-tuple-element.16), channel_id=1, source_target_pairs={{0,8},{8,16},{16,24},{24,32},{32,40},{40,48},{48,56},{56,64},{64,7... | collective-permute-start | bytes 18440 | tf_op jit(solution)/shard_map/ppermute | solution.py:495
  68.9 72.3 %collective-permute-start.1 = (f32[4,384]{1,0:T(4,128)S(1)}, f32[4,384]{1,0:T(4,128)S(1)}, u32[]{:S(2)}, u32[]{:S(2)}) collective-permute-start(f32[4,384]{1,0:T(4,128)S(1)} %get-tuple-element.17), channel_id=1, source_target_pairs={{0,120},{8,0},{16,8},{24,16},{32,24},{40,32},{48,40},{56,48},{64,5... | collective-permute-start | bytes 18440 | tf_op jit(solution)/shard_map/ppermute | solution.py:495
  110.3 51.1 %copy-start.2 = (f32[2,2,384,384]{3,2,1,0:T(8,128)S(1)}, f32[2,2,384,384]{3,2,1,0:T(8,128)}, u32[]{:S(2)}) copy-start(f32[2,2,384,384]{3,2,1,0:T(8,128)} %tile.1) | copy-start | bytes 7077892
  112.3 39.8 %all-to-all-start.2 = ((bf16[128,8,128]{2,1,0:T(8,128)(2,1)}), bf16[128,8,128]{2,1,0:T(8,128)(2,1)S(1)}, u32[]{:S(2)}, u32[]{:S(2)}) async-start(bf16[128,8,128]{2,1,0:T(8,128)(2,1)} %reshape.57), calls=%async_computation.2 | async-start | bytes 524288 | tf_op jit(solution)/shard_map/all_to_all | solution.py:508
  141.5 17.5 %collective-permute-start.3 = (f32[4,512]{1,0:T(4,128)S(1)}, f32[4,512]{1,0:T(4,128)S(1)}, u32[]{:S(2)}, u32[]{:S(2)}) collective-permute-start(f32[4,512]{1,0:T(4,128)S(1)} %pad_maximum_fusion.3), channel_id=1, source_target_pairs={{0,1},{1,2},{2,3},{3,4},{4,5},{5,6},{6,7},{7,0},{8,9},{9,10},{10,1... | collective-permute-start | bytes 24584 | tf_op jit(solution)/shard_map/ppermute | solution.py:495
  153.0 33.6 %all-to-all-start.3 = ((bf16[128,8,128]{2,1,0:T(8,128)(2,1)}), bf16[128,8,128]{2,1,0:T(8,128)(2,1)S(1)}, u32[]{:S(2)}, u32[]{:S(2)}) async-start(bf16[128,8,128]{2,1,0:T(8,128)(2,1)} %broadcast_in_dim.53), calls=%async_computation.3 | async-start | bytes 524288 | tf_op jit(solution)/shard_map/all_to_all | solution.py:513
  157.8 3.5 %collective-permute-start.2 = (f32[4,512]{1,0:T(4,128)S(1)}, f32[4,512]{1,0:T(4,128)S(1)}, u32[]{:S(2)}, u32[]{:S(2)}) collective-permute-start(f32[4,512]{1,0:T(4,128)S(1)} %pad_maximum_fusion.2), channel_id=1, source_target_pairs={{0,7},{1,0},{2,1},{3,2},{4,3},{5,4},{6,5},{7,6},{8,15},{9,8},{10,9... | collective-permute-start | bytes 24584 | tf_op jit(solution)/shard_map/ppermute | solution.py:495
  161.3 1.7 copy-start.3
  163.0 23.9 %copy-start.4 = (bf16[2,256,256]{2,1,0:T(8,128)(2,1)S(1)}, bf16[2,256,256]{2,1,0:T(8,128)(2,1)}, u32[]{:S(2)}) copy-start(bf16[2,256,256]{2,1,0:T(8,128)(2,1)} %probe.3) | copy-start | bytes 786436

commit v3 on v2

--- a/solution.py
+++ b/solution.py
@@ -301,9 +301,9 @@
 
 
 def backward_kernel(
-    wanted, tile_in, probe, tab, prop, ints, exits_in, psi_in, field_out, probe_sum, *scratch
+    wanted, tile_in, probe, tab, prop, ints, exits_in, psi_in, field_out, probe_out, *scratch
 ):
-    tile, field_a, field_b, listed, x, y, exits, psi, sems = scratch
+    tile, field_a, field_b, probe_sum, listed, x, y, exits, psi, sems = scratch
     count = list_used(wanted, listed)
     pairs = (count + 1) // 2
 
@@ -364,47 +364,64 @@
         for q in range(2):
             for k in range(3):
                 field_out[s, q, :, pl.ds(128 * k, 128)] = field_a[s, q, k] + field_b[s, q, k]
-
-
-def finish_kernel(tile, field, edge_rows, edge_cols, out, padded, flat):
+    for q in range(2):
+        for c in range(2):
+            for j in range(N // 8):
+                share = probe_sum[q, 8 * j : 8 * j + 8, 128 * c : 128 * c + 128]
+                probe_out[SHARES // 2 * q + N // 8 * c + j] = share.astype(BF16)
+
+
+def finish_kernel(tile, field, edge_rows, edge_cols, out, padded, flow_y, flow_x, flat):
     flat[...] = jnp.zeros((128, 512), F32)
     flat[0:8] = edge_cols[...]
     tall = jnp.transpose(flat[...])
     for s in range(2):
         for q in range(2):
             k = 2 * s + q
-            padded[s, q, 8 : 8 + T, 128 : 128 + T] = tile[s, q]
-            padded[s, q, 7:8, 128 : 128 + T] = edge_rows[k : k + 1]
-            padded[s, q, 8 + T : 9 + T, 128 : 128 + T] = edge_rows[4 + k : 5 + k]
-            after, before = tall[:, k : k + 1], tall[:, 4 + k : 5 + k]
-            padded[s, q, 8 : 8 + T, 128 + T : 256 + T] = jnp.broadcast_to(after[:T], (T, 128))
-            padded[s, q, 8 : 8 + T, 0:128] = jnp.broadcast_to(before[:T], (T, 128))
-            padded[s, q, 7:8, 128 + T : 256 + T] = jnp.broadcast_to(after[T : T + 1], (1, 128))
-            padded[s, q, 8 + T : 9 + T, 0:128] = jnp.broadcast_to(before[T : T + 1], (1, 128))
+            for block, side in ((0, 4 + k), (4, k)):
+                values = jnp.broadcast_to(tall[: T + 8, side : side + 1], (T + 8, 128))
+                padded[s, q, block, 8 : 8 + T] = values[:T]
+                padded[s, q, block, 0:8] = values[T:]
+                padded[s, q, block, 8 + T : 16 + T] = values[T:]
+            for c in range(3):
+                at = slice(128 * c, 128 * c + 128)
+                padded[s, q, 1 + c, 8 : 8 + T] = tile[s, q, :, at]
+                padded[s, q, 1 + c, 0:8] = jnp.broadcast_to(edge_rows[k : k + 1, at], (8, 128))
+                padded[s, q, 1 + c, 8 + T : 16 + T] = jnp.broadcast_to(
+                    edge_rows[4 + k : 5 + k, at], (8, 128)
+                )
+    high = 56
+    lane = lax.broadcasted_iota(jnp.int32, (high, 128), 1)
     for s in range(2):
-
-        def part(at, down, right):
-            here = [padded[s, q, at + 8 + down : at + 8 + down + 16, 128 + right : 128 + right + T] for q in range(2)]
-            return here
-
-        for at in range(0, T, 16):
-            here, below, right = part(at, 0, 0), part(at, 1, 0), part(at, 0, 1)
-            above, above_right = part(at, -1, 0), part(at, -1, 1)
-            left, left_below = part(at, 0, -1), part(at, 1, -1)
-
-            def slopes(one, lower, righter):
-                dy = [b - a for a, b in zip(one, lower)]
-                dx = [b - a for a, b in zip(one, righter)]
+        for at in range(0, T + 8, high):
+            for c in range(4):
+                dy, dx = [], []
+                for q in range(2):
+                    here = padded[s, q, c, at : at + high]
+                    after = padded[s, q, c + 1, at : at + high]
+                    dy.append(padded[s, q, c, at + 1 : at + 1 + high] - here)
+                    right = jnp.where(lane == 127, pltpu.roll(after, 127, 1), pltpu.roll(here, 127, 1))
+                    dx.append(right - here)
                 total = dy[0] * dy[0] + dx[0] * dx[0] + (dy[1] * dy[1] + dx[1] * dx[1])
-                return dy, dx, 1.0 / jnp.sqrt(total + tv_smooth)
-
-            dy, dx, m = slopes(here, below, right)
-            dy_up, _, m_up = slopes(above, here, above_right)
-            _, dx_left, m_left = slopes(left, left_below, here)
-            for q in range(2):
-                tv = m_up * dy_up[q] + m_left * dx_left[q] - m * dy[q] - m * dx[q]
-                grad = field[s, q, at : at + 16] + tv_weight * tv
-                out[s, q, at : at + 16] = here[q] - update_rate * grad
+                m = lax.rsqrt(total + tv_smooth)
+                for q in range(2):
+                    flow_y[s, q, c, at : at + high] = m * dy[q]
+                    flow_x[s, q, c, at : at + high] = m * dx[q]
+    high = 64
+    lane = lax.broadcasted_iota(jnp.int32, (high, 128), 1)
+    for s in range(2):
+        for q in range(2):
+            for at in range(0, T, high):
+                for c in range(1, 4):
+                    low = at + 8
+                    down = flow_y[s, q, c, low : low + high]
+                    above = flow_y[s, q, c, low - 1 : low - 1 + high]
+                    right = flow_x[s, q, c, low : low + high]
+                    before = flow_x[s, q, c - 1, low : low + high]
+                    left = jnp.where(lane == 0, pltpu.roll(before, 1, 1), pltpu.roll(right, 1, 1))
+                    to = slice(128 * c - 128, 128 * c)
+                    grad = field[s, q, at : at + high, to] + tv_weight * (above + left - down - right)
+                    out[s, q, at : at + high, to] = padded[s, q, c, low : low + high] - update_rate * grad
 
 
 VMEM = pl.BlockSpec(memory_space=pltpu.VMEM)
@@ -413,6 +430,7 @@
 SOURCES = 16
 SLOTS = SOURCES * CAP
 PAIRS = SLOTS // 2
+SHARES = 2 * N * N // (8 * 128)
 WIDE = pltpu.VMEM((2, 2, 3, T, 128), F32)
 TWO = pltpu.VMEM((2, 2, N, N), BF16)
 FRONTS = [
@@ -453,10 +471,10 @@
     tab, prop = tables()
     return pl.pallas_call(
         backward_kernel,
-        out_shape=(jax.ShapeDtypeStruct((2, 2, T, T), F32), jax.ShapeDtypeStruct((2, N, N), F32)),
+        out_shape=(jax.ShapeDtypeStruct((2, 2, T, T), F32), jax.ShapeDtypeStruct((SHARES, 8, 128), BF16)),
         in_specs=[SMEM] + [VMEM] * 5 + [HBM, HBM],
         out_specs=(VMEM, VMEM),
-        scratch_shapes=[WIDE, WIDE, WIDE, LISTED, TWO, TWO] + FRONTS,
+        scratch_shapes=[WIDE, WIDE, WIDE, pltpu.VMEM((2, N, N), F32), LISTED, TWO, TWO] + FRONTS,
         name="backward",
         **params(57),
     )(wanted, tile, probe, tab, prop, ints, exits, psi)
@@ -468,26 +486,69 @@
         out_shape=jax.ShapeDtypeStruct((2, 2, T, T), F32),
         in_specs=[VMEM] * 4,
         out_specs=VMEM,
-        scratch_shapes=[pltpu.VMEM((2, 2, T + 16, T + 256), F32), pltpu.VMEM((128, 512), F32)],
-        compiler_params=pltpu.CompilerParams(vmem_limit_bytes=24 << 20),
+        scratch_shapes=[
+            pltpu.VMEM((2, 2, 5, T + 16, 128), F32),
+            pltpu.VMEM((2, 2, 4, T + 8, 128), F32),
+            pltpu.VMEM((2, 2, 4, T + 8, 128), F32),
+            pltpu.VMEM((128, 512), F32),
+        ],
+        compiler_params=pltpu.CompilerParams(vmem_limit_bytes=32 << 20),
         name="finish",
     )(tile, field, edge_rows, edge_cols)
 
 
-def pack_kernel(slots, values, out):
+def pack_kernel(owners, corners, values, out, request, taken, wide, narrow, sems_in, sems_out):
+    group = SOURCES // 4
+
+    def arrives(g):
+        at = pl.ds(group * g, group)
+        return pltpu.make_async_copy(values.at[at], wide.at[at], sems_in.at[g])
+
+    def leaves(i, slot):
+        return pltpu.make_async_copy(narrow.at[i], out.at[slot], sems_out.at[i])
+
+    for g in range(4):
+        arrives(g).start()
+    for k in range(SOURCES):
+        taken[k] = 0
+    for k in range(2 * SLOTS):
+        request[k] = 0
+    slots = []
     for i in range(SOURCES):
-        out[slots[i]] = values[i].astype(BF16)
-
-
-def pack_call(slots, intensities):
+        rank = taken[owners[i]]
+        taken[owners[i]] = rank + 1
+        slot = owners[i] * CAP + rank
+        request[2 * slot] = corners[2 * i] + 1
+        request[2 * slot + 1] = corners[2 * i + 1] + 1
+        slots.append(slot)
+    for i in range(SOURCES):
+        if i % group == 0:
+            arrives(i // group).wait()
+        narrow[i] = wide[i].astype(BF16)
+        leaves(i, slots[i]).start()
+    for i in range(SOURCES):
+        leaves(i, slots[i]).wait()
+
+
+def pack_call(owners, corners, intensities):
     return pl.pallas_call(
         pack_kernel,
-        out_shape=jax.ShapeDtypeStruct((SLOTS, N, N), BF16),
-        in_specs=[SMEM, VMEM],
-        out_specs=VMEM,
-        compiler_params=pltpu.CompilerParams(vmem_limit_bytes=24 << 20),
+        out_shape=(
+            jax.ShapeDtypeStruct((SLOTS, N, N), BF16),
+            jax.ShapeDtypeStruct((2 * SLOTS,), jnp.int32),
+        ),
+        in_specs=[SMEM, SMEM, HBM],
+        out_specs=(HBM, SMEM),
+        scratch_shapes=[
+            pltpu.SMEM((SOURCES,), jnp.int32),
+            pltpu.VMEM((SOURCES, N, N), F32),
+            pltpu.VMEM((SOURCES, N, N), BF16),
+            pltpu.SemaphoreType.DMA((4,)),
+            pltpu.SemaphoreType.DMA((SOURCES,)),
+        ],
+        compiler_params=pltpu.CompilerParams(vmem_limit_bytes=57 << 20),
         name="pack",
-    )(slots, intensities)
+    )(owners, corners, intensities)
 
 
 def moved(x, axis, step):
@@ -495,46 +556,47 @@
     return lax.ppermute(x, axis, [(i, (i + step) % size) for i in range(size)])
 
 
-def neighbours(edge_rows, edge_cols):
+def rows_around(edge_rows, edge_cols):
     above, below = moved(edge_rows[4:], BATCH, 1), moved(edge_rows[:4], BATCH, -1)
     for_left = jnp.concatenate([edge_cols[:4], jnp.broadcast_to(above[:, :1], (4, 128))], 1)
     for_right = jnp.concatenate([edge_cols[4:], jnp.broadcast_to(below[:, -1:], (4, 128))], 1)
-    right, left = moved(for_left, TILE, -1), moved(for_right, TILE, 1)
-    return jnp.concatenate([above, below]), jnp.concatenate([right, left])
-
-
-def over_all(x):
-    devices = lax.axis_size(BATCH_TILE)
-    shares = lax.all_to_all(
-        x.astype(BF16).reshape(devices, -1, 128), BATCH_TILE, split_axis=0, concat_axis=0, tiled=True
-    )
+    return jnp.concatenate([above, below]), for_left, for_right
+
+
+def cols_around(for_left, for_right):
+    return jnp.concatenate([moved(for_left, TILE, -1), moved(for_right, TILE, 1)])
+
+
+def summed_shares(shares):
+    shares = lax.all_to_all(shares, BATCH_TILE, split_axis=0, concat_axis=0, tiled=True)
     mine = jnp.sum(shares.astype(F32), 0, keepdims=True).astype(BF16)
-    mine = jnp.broadcast_to(mine, shares.shape)
+    return jnp.broadcast_to(mine, shares.shape)
+
+
+def from_all(mine):
     total = lax.all_to_all(mine, BATCH_TILE, split_axis=0, concat_axis=0, tiled=True)
-    return total.astype(F32).reshape(x.shape)
+    return total.astype(F32).reshape(2, 2, N, 128).transpose(0, 2, 1, 3).reshape(2, N, N)
 
 
 def on_device(object_field, probe_wave, intensities, owner_rows, offsets):
-    local_rows = intensities.shape[0]
     nbatch = lax.axis_size(BATCH)
-    slots_all = nbatch * CAP
-    targets = owner_rows[:, 0]
-    serial = jnp.arange(local_rows, dtype=jnp.int32)
-    earlier = (targets[:, None] == targets[None, :]) & (serial[None, :] < serial[:, None])
-    slot_of = targets * CAP + jnp.sum(earlier.astype(jnp.int32), axis=1)
-    hit = slot_of[:, None] == jnp.arange(slots_all, dtype=jnp.int32)[None, :]
-    request = jnp.sum(jnp.where(hit[:, :, None], offsets[:, None, :] + 1, 0), axis=0)
+    sent, request = pack_call(owner_rows.reshape(-1), offsets.reshape(-1), intensities)
+    sent, request = lax.optimization_barrier((sent, request))
     wanted = lax.all_to_all(
         request.reshape(nbatch, CAP * 2), BATCH, split_axis=0, concat_axis=0, tiled=True
-    ).reshape(slots_all * 2)
-    sent = pack_call(slot_of, intensities).reshape(nbatch, CAP, N, N)
+    ).reshape(SLOTS * 2)
+    sent, wanted = lax.optimization_barrier((sent.reshape(nbatch, CAP, N, N), wanted))
     ints = lax.all_to_all(sent, BATCH, split_axis=0, concat_axis=0, tiled=True)
-    ints = ints.reshape(slots_all, N, N)
+    ints = ints.reshape(SLOTS, N, N)
     exits, psi, edge_rows, edge_cols = forward_call(wanted, object_field, probe_wave)
-    around = neighbours(edge_rows, edge_cols)
-    field_grad, probe_local = backward_call(wanted, object_field, probe_wave, ints, exits, psi)
-    probe_total = over_all(probe_local)
-    new_object = finish_call(object_field, field_grad, *around)
+    rows, *columns = rows_around(edge_rows, edge_cols)
+    wanted, columns = lax.optimization_barrier((wanted, columns))
+    columns = cols_around(*columns)
+    field_grad, probe_shares = backward_call(wanted, object_field, probe_wave, ints, exits, psi)
+    mine = summed_shares(probe_shares)
+    new_object = finish_call(object_field, field_grad, rows, columns)
+    mine, new_object = lax.optimization_barrier((mine, new_object))
+    probe_total = from_all(mine)
     new_probe = probe_wave.astype(F32) - probe_rate * probe_total
     return (new_object, new_probe)
 

time: 190 us -> 179 us (0.942)
  starting transfers between devices: 72 us -> 50.3 us
  waiting for transfers between devices: 26.8 us -> 47.7 us
  Pallas kernels: 70.7 us -> 55.7 us
  blocking collectives: 0 us -> 13.8 us
  other arithmetic: 6.03 us -> 0.93 us
  local copies, waits for them, and re-layouts: 11.4 us -> 8.92 us
    ppermute x4, waiting for transfers between devices: 2.32 us -> 34.4 us  [moved(): return lax.ppermute(x, axis, [(i, (i + step) % size) for i in range(size)])]
    ppermute x4, starting transfers between devices: 24.9 us -> 4.15 us  [moved(): return lax.ppermute(x, axis, [(i, (i + step) % size) for i in range(size)])]
    pallas_call x1, Pallas kernels: 23.7 us -> 4.95 us  [finish_call(): pl.pallas_call(finish_kernel, out_shape=jax.ShapeDtypeStruct((2, 2, T, T)...]
    all_to_all x0 -> x1, blocking collectives: none -> 13.8 us  [on_device(): lax.all_to_all(request.reshape(nbatch, CAP * 2), BATCH, split_axis=0, con...]
    all_to_all x1, waiting for transfers between devices: 15 us -> 2.55 us  [on_device(): ints = lax.all_to_all(sent, BATCH, split_axis=0, concat_axis=0, tiled=True)]
    pallas_call x1, Pallas kernels: 0.74 us -> 4.39 us  [pack_call(): pl.pallas_call(pack_kernel, out_shape=(jax.ShapeDtypeStruct((SLOTS, N, N)...]
    unnamed x10 -> x9, local copies, waits for them, and re-layouts: 5.8 us -> 3.56 us
    add x3 -> x0, other arithmetic: 2 us -> none  [the longest x2 1.32 us: on_device(): slot_of = targets * CAP + jnp.sum(earlier.astype(jnp.int32), axis=1)]
  transfers between devices with their start and end apart: 8 -> 7, of which waited for: 4 -> 5; matrix products, arithmetic and copies ran while one was open for 4% -> 1% of each run, Pallas kernels for 38% -> 14%
where the time goes in v3:
time: 179 us; the launch traced here: 178 us
  Pallas kernels  55.7 us (31%)
  starting transfers between devices  50.3 us (28%)
  waiting for transfers between devices  47.7 us (27%)
  blocking collectives  13.8 us (8%)
  local copies, waits for them, and re-layouts  8.92 us (5%)
    ppermute x4, waiting for transfers between devices, moved(): return lax.ppermute(x, axis, [(i, (i + step) % size) for i in range(size)])  34.4 us
    all_to_all x1, starting transfers between devices, summed_shares(): lax.all_to_all(shares, BATCH_TILE, split_axis=0, concat_axis=0, tiled=True)  31.6 us
    pallas_call x1, Pallas kernels, backward_call(): pl.pallas_call(backward_kernel, out_shape=(jax.ShapeDtypeStruct((2, 2, T,...  25.7 us
    pallas_call x1, Pallas kernels, forward_call(): pl.pallas_call(forward_kernel, out_shape=(jax.ShapeDtypeStruct((PAIRS, 2,...  20.7 us
    all_to_all x1, blocking collectives, on_device(): lax.all_to_all(request.reshape(nbatch, CAP * 2), BATCH, split_axis=0, con...  13.8 us
    all_to_all x1, waiting for transfers between devices, from_all(): lax.all_to_all(mine, BATCH_TILE, split_axis=0, concat_axis=0, tiled=True)  10.7 us
    all_to_all x1, starting transfers between devices, from_all(): lax.all_to_all(mine, BATCH_TILE, split_axis=0, concat_axis=0, tiled=True)  10 us
    pallas_call x1, Pallas kernels, finish_call(): pl.pallas_call(finish_kernel, out_shape=jax.ShapeDtypeStruct((2, 2, T, T)...  4.95 us
  transfers between devices with their start and end apart: 7, of which 5 were waited for; matrix products, arithmetic and copies ran while one was open for 1% of the time, Pallas kernels for 14%

profile of v3, /device:TPU:1, one launch (start us, length us, event | category | flops | bytes accessed | tf_op | source)
XLA Modules:
  0.0 178.2 jit_solution(4380250820078769978)
XLA Ops:
  0.6 0.8 copy.17
  1.4 0.6 reshape.35.corners
  2.0 4.4 %pack.1 = (bf16[32,256,256]{2,1,0:T(8,128)(2,1)}, s32[64]{0:T(128)}) custom-call(s32[16]{0:T(128)} %bitcast.12, s32[32]{0:T(128)} %reshape.35.corners, f32[16,256,256]{2,1,0:T(8,128)} %values.1), custom_call_target="tpu_custom_call" | custom-call | tf_op jit(solution)/shard_map/pack/pallas_call | solution.py:534
  6.4 0.7 all_to_all.15
  7.1 13.8 %all_to_all.24 = s32[16,1,4]{2,1,0:T(1,128)S(1)} all-to-all(s32[16,1,4]{2,1,0:T(1,128)S(1)} %bitcast.11), channel_id=1, replica_groups=mesh['batch_0'=4,'batch_1'=4,'tile_0'=4,'tile_1'=2] {'batch_0','batch_1'}, dimensions={0} | all-to-all | bytes 512 | tf_op jit(solution)/shard_map/all_to_all | solution.py:585
  21.5 0.7 reduce.8
  22.7 4.6 %all-to-all-start.1 = ((bf16[16,2,256,256]{3,2,1,0:T(8,128)(2,1)}), bf16[16,2,256,256]{3,2,1,0:T(8,128)(2,1)}, u32[]{:S(2)}, u32[]{:S(2)}) async-start(bf16[16,2,256,256]{3,2,1,0:T(8,128)(2,1)} %bitcast.9), calls=%async_computation.1 | async-start | bytes 8388608 | tf_op jit(solution)/shard_map/all_to_all | solution.py:589
  27.3 20.7 %forward.1 = (f32[16,2,2,256,256]{4,3,2,1,0:T(8,128)}, bf16[16,2,2,256,256]{4,3,2,1,0:T(8,128)(2,1)}, f32[8,384]{1,0:T(8,128)}, f32[8,384]{1,0:T(8,128)}) custom-call(s32[64]{0:T(128)} %reshape.37.wanted, f32[2,2,384,384]{3,2,1,0:T(8,128)} %tile.1, bf16[2,256,256]{2,1,0:T(8,128)(2,1)} %probe.3, bf16[3,256,256]{2,1,0:T(8,128)(2,1)} %constant.9.clone.tab, ...), custom_call_target="tpu_custom_call" | custom-call | flops 25769803776 | bytes 33554432 | tf_op jit(solution)/shard_map/forward/pallas_call | solution.py:454
  48.0 0.8 fusion.1
  48.8 2.4 %collective-permute-start.1 = (f32[4,384]{1,0:T(4,128)S(1)}, f32[4,384]{1,0:T(4,128)S(1)}, u32[]{:S(2)}, u32[]{:S(2)}) collective-permute-start(f32[4,384]{1,0:T(4,128)S(1)} %get-tuple-element.38), channel_id=1, source_target_pairs={{0,120},{8,0},{16,8},{24,16},{32,24},{40,32},{48,40},{56,48},{64,5... | collective-permute-start | bytes 18440 | tf_op jit(solution)/shard_map/ppermute | solution.py:556
  51.2 0.8 fusion
  51.9 31.9 %collective-permute-done.1 = f32[4,384]{1,0:T(4,128)S(1)} collective-permute-done((f32[4,384]{1,0:T(4,128)S(1)}, f32[4,384]{1,0:T(4,128)S(1)}, u32[]{:S(2)}, u32[]{:S(2)}) %collective-permute-start.1) | collective-permute-done | bytes 6176 | tf_op jit(solution)/shard_map/ppermute | solution.py:556
  84.3 2.6 %all-to-all-done.1 = bf16[16,2,256,256]{3,2,1,0:T(8,128)(2,1)} async-done(((bf16[16,2,256,256]{3,2,1,0:T(8,128)(2,1)}), bf16[16,2,256,256]{3,2,1,0:T(8,128)(2,1)}, u32[]{:S(2)}, u32[]{:S(2)}) %all-to-all-start.1) | async-done | bytes 4194336 | tf_op jit(solution)/shard_map/all_to_all | solution.py:589
  86.8 25.7 %backward.1 = (f32[2,2,384,384]{3,2,1,0:T(8,128)}, bf16[128,8,128]{2,1,0:T(8,128)(2,1)}) custom-call(s32[64]{0:T(128)} %reshape.37.wanted, f32[2,2,384,384]{3,2,1,0:T(8,128)} %tile.1, bf16[2,256,256]{2,1,0:T(8,128)(2,1)} %probe.3, bf16[3,256,256]{2,1,0:T(8,128)(2,1)} %constant.9.clone.tab, f32[2,256,256]{2,1,0:T(8,128)} %constant.10.clone.prop, ...), custom_call_target="tpu_custom_call" | custom-call | flops 25769803776 | bytes 33554432 | tf_op jit(solution)/shard_map/backward/pallas_call | solution.py:472
  112.5 31.6 %all-to-all-start.2 = ((bf16[128,8,128]{2,1,0:T(8,128)(2,1)}), bf16[128,8,128]{2,1,0:T(8,128)(2,1)S(1)}, u32[]{:S(2)}, u32[]{:S(2)}) async-start(bf16[128,8,128]{2,1,0:T(8,128)(2,1)} %get-tuple-element.26), calls=%async_computation.2 | async-start | bytes 524288 | tf_op jit(solution)/shard_map/all_to_all | solution.py:571
  144.1 1.3 collective-permute-start.2
  145.9 1.8 %collective-permute-done.2 = f32[4,512]{1,0:T(4,128)S(1)} collective-permute-done((f32[4,512]{1,0:T(4,128)S(1)}, f32[4,512]{1,0:T(4,128)S(1)}, u32[]{:S(2)}, u32[]{:S(2)}) %collective-permute-start.2) | collective-permute-done | bytes 8224 | tf_op jit(solution)/shard_map/ppermute | solution.py:556
  147.7 0.7 collective-permute-done.3
  148.5 1.7 copy-done.1
  150.1 5.0 %finish.1 = f32[2,2,384,384]{3,2,1,0:T(8,128)} custom-call(f32[2,2,384,384]{3,2,1,0:T(8,128)S(1)} %copy-done, f32[2,2,384,384]{3,2,1,0:T(8,128)S(1)} %copy-done.1, f32[8,384]{1,0:T(8,128)S(1)} %pad_maximum_fusion.1.edge_rows, f32[8,512]{1,0:T(8,128)S(1)} %pad_maximum_fusion.edge_cols), custom_call_target="tpu_custom_call" | custom-call | tf_op jit(solution)/shard_map/finish/pallas_call | solution.py:484
  155.2 0.7 broadcast_in_dim.24
  155.9 10.0 %all-to-all-start.3 = ((bf16[128,8,128]{2,1,0:T(8,128)(2,1)}), bf16[128,8,128]{2,1,0:T(8,128)(2,1)S(1)}, u32[]{:S(2)}, u32[]{:S(2)}) async-start(bf16[128,8,128]{2,1,0:T(8,128)(2,1)} %broadcast_in_dim.24), calls=%async_computation.3 | async-start | bytes 524288 | tf_op jit(solution)/shard_map/all_to_all | solution.py:577
  166.1 10.7 %all-to-all-done.3 = bf16[128,8,128]{2,1,0:T(8,128)(2,1)S(1)} async-done(((bf16[128,8,128]{2,1,0:T(8,128)(2,1)}), bf16[128,8,128]{2,1,0:T(8,128)(2,1)S(1)}, u32[]{:S(2)}, u32[]{:S(2)}) %all-to-all-start.3) | async-done | bytes 262176 | tf_op jit(solution)/shard_map/all_to_all | solution.py:577
  177.2 1.0 copy.21
  (23 shorter events, 2.7 us)
Async XLA Ops:
  22.7 64.1 %all-to-all-start.1 = ((bf16[16,2,256,256]{3,2,1,0:T(8,128)(2,1)}), bf16[16,2,256,256]{3,2,1,0:T(8,128)(2,1)}, u32[]{:S(2)}, u32[]{:S(2)}) async-start(bf16[16,2,256,256]{3,2,1,0:T(8,128)(2,1)} %bitcast.9), calls=%async_computation.1 | async-start | bytes 8388608 | tf_op jit(solution)/shard_map/all_to_all | solution.py:589
  48.8 35.0 %collective-permute-start.1 = (f32[4,384]{1,0:T(4,128)S(1)}, f32[4,384]{1,0:T(4,128)S(1)}, u32[]{:S(2)}, u32[]{:S(2)}) collective-permute-start(f32[4,384]{1,0:T(4,128)S(1)} %get-tuple-element.38), channel_id=1, source_target_pairs={{0,120},{8,0},{16,8},{24,16},{32,24},{40,32},{48,40},{56,48},{64,5... | collective-permute-start | bytes 18440 | tf_op jit(solution)/shard_map/ppermute | solution.py:556
  51.9 32.1 %collective-permute-start = (f32[4,384]{1,0:T(4,128)S(1)}, f32[4,384]{1,0:T(4,128)S(1)}, u32[]{:S(2)}, u32[]{:S(2)}) collective-permute-start(f32[4,384]{1,0:T(4,128)S(1)} %get-tuple-element.39), channel_id=1, source_target_pairs={{0,8},{8,16},{16,24},{24,32},{32,40},{40,48},{48,56},{56,64},{64,7... | collective-permute-start | bytes 18440 | tf_op jit(solution)/shard_map/ppermute | solution.py:556
  86.8 61.6 %copy-start = (f32[2,2,384,384]{3,2,1,0:T(8,128)S(1)}, f32[2,2,384,384]{3,2,1,0:T(8,128)}, u32[]{:S(2)}) copy-start(f32[2,2,384,384]{3,2,1,0:T(8,128)} %tile.1) | copy-start | bytes 7077892
  112.5 53.5 %copy-start.2 = (bf16[2,256,256]{2,1,0:T(8,128)(2,1)S(1)}, bf16[2,256,256]{2,1,0:T(8,128)(2,1)}, u32[]{:S(2)}) copy-start(bf16[2,256,256]{2,1,0:T(8,128)(2,1)} %probe.3) | copy-start | bytes 786436
  112.5 42.6 %all-to-all-start.2 = ((bf16[128,8,128]{2,1,0:T(8,128)(2,1)}), bf16[128,8,128]{2,1,0:T(8,128)(2,1)S(1)}, u32[]{:S(2)}, u32[]{:S(2)}) async-start(bf16[128,8,128]{2,1,0:T(8,128)(2,1)} %get-tuple-element.26), calls=%async_computation.2 | async-start | bytes 524288 | tf_op jit(solution)/shard_map/all_to_all | solution.py:571
  144.1 3.6 %collective-permute-start.2 = (f32[4,512]{1,0:T(4,128)S(1)}, f32[4,512]{1,0:T(4,128)S(1)}, u32[]{:S(2)}, u32[]{:S(2)}) collective-permute-start(f32[4,512]{1,0:T(4,128)S(1)} %get-tuple-element.28), channel_id=1, source_target_pairs={{0,7},{1,0},{2,1},{3,2},{4,3},{5,4},{6,5},{7,6},{8,15},{9,8},{10,9... | collective-permute-start | bytes 24584 | tf_op jit(solution)/shard_map/ppermute | solution.py:556
  145.4 3.1 %collective-permute-start.3 = (f32[4,512]{1,0:T(4,128)S(1)}, f32[4,512]{1,0:T(4,128)S(1)}, u32[]{:S(2)}, u32[]{:S(2)}) collective-permute-start(f32[4,512]{1,0:T(4,128)S(1)} %get-tuple-element.29), channel_id=1, source_target_pairs={{0,1},{1,2},{2,3},{3,4},{4,5},{5,6},{6,7},{7,0},{8,9},{9,10},{10,1... | collective-permute-start | bytes 24584 | tf_op jit(solution)/shard_map/ppermute | solution.py:556
  148.4 1.7 copy-start.1
  155.9 20.9 %all-to-all-start.3 = ((bf16[128,8,128]{2,1,0:T(8,128)(2,1)}), bf16[128,8,128]{2,1,0:T(8,128)(2,1)S(1)}, u32[]{:S(2)}, u32[]{:S(2)}) async-start(bf16[128,8,128]{2,1,0:T(8,128)(2,1)} %broadcast_in_dim.24), calls=%async_computation.3 | async-start | bytes 524288 | tf_op jit(solution)/shard_map/all_to_all | solution.py:577

commit v4 on v3

--- a/solution.py
+++ b/solution.py
@@ -34,7 +34,16 @@
     squared = (freq * freq).astype(np.float64)
     phases = -(0.5 / N) * (squared[:, None] + squared[None, :])
     prop = np.stack([np.cos(phases), np.sin(phases)]).astype(np.float32)
-    return np.stack([cos_table, sin_table, -sin_table]), prop
+    return np.stack([cos_table, sin_table, -sin_table]), prop, halves(cos_table, sin_table)
+
+
+def halves(cos_table, sin_table):
+    out = []
+    for sin in (sin_table, -sin_table):
+        for odd in range(2):
+            c, d = cos_table[: N // 2, odd::2], sin[: N // 2, odd::2]
+            out.append(np.block([[c, -d], [d, c]]))
+    return np.stack(out)
 
 
 def rows(j):
@@ -52,7 +61,7 @@
                 )
 
 
-def shared(start, acc, x, y, tab):
+def shared(start, acc, x, y, tab, half):
     row, col = start
     regs = (0, 1)
     lane = lax.broadcasted_iota(jnp.int32, (R, 128), 1)
@@ -62,22 +71,30 @@
     moved = lane >= col
 
     def left(forward):
-        sin, neg = (1, 2) if forward else (2, 1)
-        xr, xi = x[0], x[1]
-        issue(
-            acc,
-            regs,
-            ((xr[...], xi[...]), (xr[...], xi[...])),
-            (
-                (lambda j: tab[0, rows(j)], lambda j: tab[neg, rows(j)]),
-                (lambda j: tab[sin, rows(j)], lambda j: tab[0, rows(j)]),
-            ),
-        )
+        for odd in range(2):
+            part = [
+                jnp.concatenate([x[q, c, pl.ds(odd, N // 2, stride=2), :] for c in range(2)], 1)
+                for q in range(2)
+            ]
+            pltpu.matmul_push_rhs(
+                jnp.concatenate(part, 0).astype(BF16), staging_register=0, mxu_index=odd
+            )
+        for j in range(PIECES):
+            for odd in range(2):
+                lhs = half[(0 if forward else 2) + odd, rows(j)]
+                pltpu.matmul_acc_lhs(acc[odd][j], lhs, load_staged_rhs=0 if j == 0 else None)
 
     def middle():
-        for j in range(PIECES):
+        for j in range(PIECES // 2):
             for q in range(2):
-                y[q][rows(j)] = pltpu.matmul_pop(acc[q][j]).astype(BF16)
+                even = pltpu.matmul_pop(acc[0][PIECES // 2 * q + j])
+                odd = pltpu.matmul_pop(acc[1][PIECES // 2 * q + j])
+                y[q][rows(j)] = (even + odd).astype(BF16)
+                y[q][rows(PIECES // 2 + j)] = (even - odd).astype(BF16)
+
+    def keep_x(q, j, value):
+        for c in range(2):
+            x[q, c, rows(j)] = value[:, 128 * c : 128 * c + 128]
 
     def right(forward):
         sin, neg = (1, 2) if forward else (2, 1)
@@ -111,23 +128,23 @@
             fr, fi = pops(j)
             hr, hi = prop[0, rows(j)], prop[1, rows(j)]
             if sign > 0:
-                x[0][rows(j)] = (hr * fr - hi * fi).astype(BF16)
-                x[1][rows(j)] = (hr * fi + hi * fr).astype(BF16)
+                keep_x(0, j, hr * fr - hi * fi)
+                keep_x(1, j, hr * fi + hi * fr)
             else:
-                x[0][rows(j)] = (hr * fr + hi * fi).astype(BF16)
-                x[1][rows(j)] = (hr * fi - hi * fr).astype(BF16)
-
-    return left, middle, right, pops, cut, put, kick
+                keep_x(0, j, hr * fr + hi * fi)
+                keep_x(1, j, hr * fi - hi * fr)
+
+    return left, middle, right, pops, cut, put, kick, keep_x
 
 
 def forward_steps(env, start, acc, x, y, psi, exits):
-    tile, probe, tab, prop = env
-    left, middle, right, pops, cut, _, kick = shared(start, acc, x, y, tab)
+    tile, probe, tab, prop, half = env
+    left, middle, right, pops, cut, _, kick, keep_x = shared(start, acc, x, y, tab, half)
     for j in range(PIECES):
         tr, ti = cut(tile, 0, 0, j), cut(tile, 0, 1, j)
         pr, pi = probe[0, rows(j)].astype(F32), probe[1, rows(j)].astype(F32)
-        x[0][rows(j)] = (pr * tr - pi * ti).astype(BF16)
-        x[1][rows(j)] = (pr * ti + pi * tr).astype(BF16)
+        keep_x(0, j, pr * tr - pi * ti)
+        keep_x(1, j, pr * ti + pi * tr)
     left(True)
     yield
     middle()
@@ -146,8 +163,8 @@
         psi[1, rows(j)] = wi
         wr, wi = wr.astype(F32), wi.astype(F32)
         tr, ti = cut(tile, 1, 0, j), cut(tile, 1, 1, j)
-        x[0][rows(j)] = (wr * tr - wi * ti).astype(BF16)
-        x[1][rows(j)] = (wr * ti + wi * tr).astype(BF16)
+        keep_x(0, j, wr * tr - wi * ti)
+        keep_x(1, j, wr * ti + wi * tr)
     left(True)
     yield
     middle()
@@ -160,13 +177,13 @@
 
 
 def backward_steps(env, start, scale, ints, acc, x, y, psi, exits, field):
-    tile, probe, tab, prop, probe_sum = env
-    left, middle, right, pops, cut, put, kick = shared(start, acc, x, y, tab)
+    tile, probe, tab, prop, half, probe_sum = env
+    left, middle, right, pops, cut, put, kick, keep_x = shared(start, acc, x, y, tab, half)
     for j in range(PIECES):
         er, ei = exits[0, rows(j)], exits[1, rows(j)]
         misfit = scale * (er * er + ei * ei - ints[rows(j)].astype(F32))
-        x[0][rows(j)] = (misfit * er).astype(BF16)
-        x[1][rows(j)] = (misfit * ei).astype(BF16)
+        keep_x(0, j, misfit * er)
+        keep_x(1, j, misfit * ei)
     left(False)
     yield
     middle()
@@ -176,8 +193,8 @@
         gr, gi = pops(j)
         wr, wi = psi[0, rows(j)].astype(F32), psi[1, rows(j)].astype(F32)
         tr, ti = cut(tile, 1, 0, j), cut(tile, 1, 1, j)
-        x[0][rows(j)] = (gr * tr + gi * ti).astype(BF16)
-        x[1][rows(j)] = (gi * tr - gr * ti).astype(BF16)
+        keep_x(0, j, gr * tr + gi * ti)
+        keep_x(1, j, gi * tr - gr * ti)
         put(field, 1, 0, j, gr * wr + gi * wi)
         put(field, 1, 1, j, gi * wr - gr * wi)
     left(False)
@@ -242,7 +259,7 @@
 
 
 def forward_kernel(
-    wanted, tile_in, probe, tab, prop, exits_out, psi_out, edge_rows, edge_cols, tile, listed, x, y, exits, psi, sems
+    wanted, tile_in, probe, tab, prop, half, exits_out, psi_out, edge_rows, edge_cols, tile, listed, x, y, exits, psi, sems
 ):
     round_tile(tile_in, tile)
     for s in range(2):
@@ -252,7 +269,7 @@
             edge_rows[4 + k : 5 + k] = tile_in[s, q, T - 1 : T, :]
             edge_cols[k : k + 1] = jnp.transpose(tile_in[s, q, :, 0:128])[0:1]
             edge_cols[4 + k : 5 + k] = jnp.transpose(tile_in[s, q, :, T - 128 : T])[127:128]
-    env = (tile, probe, tab, prop)
+    env = (tile, probe, tab, prop, half)
     count = list_used(wanted, listed)
     pairs = (count + 1) // 2
 
@@ -279,7 +296,7 @@
                         env,
                         at[i],
                         (acc_a, acc_b)[i],
-                        (x.at[i, 0], x.at[i, 1]),
+                        x.at[i],
                         (y.at[i, 0], y.at[i, 1]),
                         psi.at[b, i],
                         exits.at[b, i],
@@ -301,7 +318,7 @@
 
 
 def backward_kernel(
-    wanted, tile_in, probe, tab, prop, ints, exits_in, psi_in, field_out, probe_out, *scratch
+    wanted, tile_in, probe, tab, prop, half, ints, exits_in, psi_in, field_out, probe_out, *scratch
 ):
     tile, field_a, field_b, probe_sum, listed, x, y, exits, psi, sems = scratch
     count = list_used(wanted, listed)
@@ -325,7 +342,7 @@
                 for k in range(3):
                     field[s, q, k] = jnp.zeros((T, 128), F32)
     probe_sum[...] = jnp.zeros((2, N, N), F32)
-    env = (tile, probe, tab, prop, probe_sum)
+    env = (tile, probe, tab, prop, half, probe_sum)
 
     def body(acc_a, acc_b):
         @pl.loop(0, pairs)
@@ -349,7 +366,7 @@
                         scales[i],
                         ints.at[slots[i]],
                         (acc_a, acc_b)[i],
-                        (x.at[i, 0], x.at[i, 1]),
+                        x.at[i],
                         (y.at[i, 0], y.at[i, 1]),
                         psi.at[b, i],
                         exits.at[b, i],
@@ -438,6 +455,7 @@
     pltpu.VMEM((2, 2, 2, N, N), BF16),
     pltpu.SemaphoreType.DMA((2, 2)),
 ]
+SPLIT = pltpu.VMEM((2, 2, 2, N, 128), F32)
 LISTED = pltpu.SMEM((SLOTS + 1,), jnp.int32)
 
 
@@ -450,7 +468,7 @@
 
 
 def forward_call(wanted, tile, probe):
-    tab, prop = tables()
+    tab, prop, half = tables()
     return pl.pallas_call(
         forward_kernel,
         out_shape=(
@@ -459,25 +477,25 @@
             jax.ShapeDtypeStruct((8, T), F32),
             jax.ShapeDtypeStruct((8, T), F32),
         ),
-        in_specs=[SMEM] + [VMEM] * 4,
+        in_specs=[SMEM] + [VMEM] * 5,
         out_specs=(HBM, HBM, VMEM, VMEM),
-        scratch_shapes=[WIDE, LISTED, TWO, TWO] + FRONTS,
+        scratch_shapes=[WIDE, LISTED, SPLIT, TWO] + FRONTS,
         name="forward",
         **params(57),
-    )(wanted, tile, probe, tab, prop)
+    )(wanted, tile, probe, tab, prop, half)
 
 
 def backward_call(wanted, tile, probe, ints, exits, psi):
-    tab, prop = tables()
+    tab, prop, half = tables()
     return pl.pallas_call(
         backward_kernel,
         out_shape=(jax.ShapeDtypeStruct((2, 2, T, T), F32), jax.ShapeDtypeStruct((SHARES, 8, 128), BF16)),
-        in_specs=[SMEM] + [VMEM] * 5 + [HBM, HBM],
+        in_specs=[SMEM] + [VMEM] * 6 + [HBM, HBM],
         out_specs=(VMEM, VMEM),
-        scratch_shapes=[WIDE, WIDE, WIDE, pltpu.VMEM((2, N, N), F32), LISTED, TWO, TWO] + FRONTS,
+        scratch_shapes=[WIDE, WIDE, WIDE, pltpu.VMEM((2, N, N), F32), LISTED, SPLIT, TWO] + FRONTS,
         name="backward",
         **params(57),
-    )(wanted, tile, probe, tab, prop, ints, exits, psi)
+    )(wanted, tile, probe, tab, prop, half, ints, exits, psi)
 
 
 def finish_call(tile, field, edge_rows, edge_cols):
@@ -497,50 +515,62 @@
     )(tile, field, edge_rows, edge_cols)
 
 
-def pack_kernel(owners, corners, values, out, request, taken, wide, narrow, sems_in, sems_out):
-    group = SOURCES // 4
-
-    def arrives(g):
-        at = pl.ds(group * g, group)
-        return pltpu.make_async_copy(values.at[at], wide.at[at], sems_in.at[g])
-
-    def leaves(i, slot):
-        return pltpu.make_async_copy(narrow.at[i], out.at[slot], sems_out.at[i])
-
-    for g in range(4):
-        arrives(g).start()
+def route_kernel(owners, corners, request, slots, taken):
     for k in range(SOURCES):
         taken[k] = 0
     for k in range(2 * SLOTS):
         request[k] = 0
-    slots = []
     for i in range(SOURCES):
         rank = taken[owners[i]]
         taken[owners[i]] = rank + 1
         slot = owners[i] * CAP + rank
         request[2 * slot] = corners[2 * i] + 1
         request[2 * slot + 1] = corners[2 * i + 1] + 1
-        slots.append(slot)
+        slots[i] = slot
+
+
+def route_call(owners, corners):
+    return pl.pallas_call(
+        route_kernel,
+        out_shape=(
+            jax.ShapeDtypeStruct((2 * SLOTS,), jnp.int32),
+            jax.ShapeDtypeStruct((SOURCES,), jnp.int32),
+        ),
+        in_specs=[SMEM, SMEM],
+        out_specs=(SMEM, SMEM),
+        scratch_shapes=[pltpu.SMEM((SOURCES,), jnp.int32)],
+        name="route",
+    )(owners, corners)
+
+
+def pack_kernel(slots, values, out, wide, narrow, sems_in, sems_out):
+    group = SOURCES // 4
+
+    def arrives(g):
+        at = pl.ds(group * g, group)
+        return pltpu.make_async_copy(values.at[at], wide.at[at], sems_in.at[g])
+
+    def leaves(i):
+        return pltpu.make_async_copy(narrow.at[i], out.at[slots[i]], sems_out.at[i])
+
+    for g in range(4):
+        arrives(g).start()
     for i in range(SOURCES):
         if i % group == 0:
             arrives(i // group).wait()
         narrow[i] = wide[i].astype(BF16)
-        leaves(i, slots[i]).start()
+        leaves(i).start()
     for i in range(SOURCES):
-        leaves(i, slots[i]).wait()
-
-
-def pack_call(owners, corners, intensities):
+        leaves(i).wait()
+
+
+def pack_call(slots, intensities):
     return pl.pallas_call(
         pack_kernel,
-        out_shape=(
-            jax.ShapeDtypeStruct((SLOTS, N, N), BF16),
-            jax.ShapeDtypeStruct((2 * SLOTS,), jnp.int32),
-        ),
-        in_specs=[SMEM, SMEM, HBM],
-        out_specs=(HBM, SMEM),
+        out_shape=jax.ShapeDtypeStruct((SLOTS, N, N), BF16),
+        in_specs=[SMEM, HBM],
+        out_specs=HBM,
         scratch_shapes=[
-            pltpu.SMEM((SOURCES,), jnp.int32),
             pltpu.VMEM((SOURCES, N, N), F32),
             pltpu.VMEM((SOURCES, N, N), BF16),
             pltpu.SemaphoreType.DMA((4,)),
@@ -548,7 +578,7 @@
         ],
         compiler_params=pltpu.CompilerParams(vmem_limit_bytes=57 << 20),
         name="pack",
-    )(owners, corners, intensities)
+    )(slots, intensities)
 
 
 def moved(x, axis, step):
@@ -580,12 +610,11 @@
 
 def on_device(object_field, probe_wave, intensities, owner_rows, offsets):
     nbatch = lax.axis_size(BATCH)
-    sent, request = pack_call(owner_rows.reshape(-1), offsets.reshape(-1), intensities)
-    sent, request = lax.optimization_barrier((sent, request))
+    request, slots = route_call(owner_rows.reshape(-1), offsets.reshape(-1))
     wanted = lax.all_to_all(
         request.reshape(nbatch, CAP * 2), BATCH, split_axis=0, concat_axis=0, tiled=True
     ).reshape(SLOTS * 2)
-    sent, wanted = lax.optimization_barrier((sent.reshape(nbatch, CAP, N, N), wanted))
+    sent = pack_call(slots, intensities).reshape(nbatch, CAP, N, N)
     ints = lax.all_to_all(sent, BATCH, split_axis=0, concat_axis=0, tiled=True)
     ints = ints.reshape(SLOTS, N, N)
     exits, psi, edge_rows, edge_cols = forward_call(wanted, object_field, probe_wave)

time: 179 us -> 174 us (0.972)
  blocking collectives: 13.8 us -> 0 us
  starting transfers between devices: 50.3 us -> 62.3 us
  waiting for transfers between devices: 47.7 us -> 44.2 us
    all_to_all x1 -> x0, blocking collectives: 13.8 us -> none  [on_device(): lax.all_to_all(request.reshape(nbatch, CAP * 2), BATCH, split_axis=0, con...]
    all_to_all x0 -> x1, starting transfers between devices: none -> 7.57 us  [on_device(): lax.all_to_all(request.reshape(nbatch, CAP * 2), BATCH, split_axis=0, con...]
    ppermute x4, waiting for transfers between devices: 34.4 us -> 28.4 us  [moved(): return lax.ppermute(x, axis, [(i, (i + step) % size) for i in range(size)])]
    ppermute x4, starting transfers between devices: 4.15 us -> 8.6 us  [moved(): return lax.ppermute(x, axis, [(i, (i + step) % size) for i in range(size)])]
    all_to_all x0 -> x1, waiting for transfers between devices: none -> 2.5 us  [on_device(): lax.all_to_all(request.reshape(nbatch, CAP * 2), BATCH, split_axis=0, con...]
    pallas_call x1 -> x2, Pallas kernels: 4.39 us -> 5.16 us  [the longest x1 3.85 us: pack_call(): pl.pallas_call(pack_kernel, out_shape=jax.ShapeDtypeStruct((SLOTS, N, N),...]
  transfers between devices with their start and end apart: 7 -> 8, of which waited for: 5 -> 6; matrix products, arithmetic and copies ran while one was open for 1% -> 2% of each run, Pallas kernels for 14% -> 17%
where the time goes in v4:
time: 174 us; the launch traced here: 173 us
  starting transfers between devices  62.3 us (36%)
  Pallas kernels  55.6 us (32%)
  waiting for transfers between devices  44.2 us (25%)
  local copies, waits for them, and re-layouts  9.53 us (5%)
    all_to_all x1, starting transfers between devices, summed_shares(): lax.all_to_all(shares, BATCH_TILE, split_axis=0, concat_axis=0, tiled=True)  31.6 us
    ppermute x4, waiting for transfers between devices, moved(): return lax.ppermute(x, axis, [(i, (i + step) % size) for i in range(size)])  28.4 us
    pallas_call x1, Pallas kernels, backward_call(): pl.pallas_call(backward_kernel, out_shape=(jax.ShapeDtypeStruct((2, 2, T,...  25.1 us
    pallas_call x1, Pallas kernels, forward_call(): pl.pallas_call(forward_kernel, out_shape=(jax.ShapeDtypeStruct((PAIRS, 2,...  20.4 us
    all_to_all x1, waiting for transfers between devices, from_all(): lax.all_to_all(mine, BATCH_TILE, split_axis=0, concat_axis=0, tiled=True)  10.7 us
    all_to_all x1, starting transfers between devices, from_all(): lax.all_to_all(mine, BATCH_TILE, split_axis=0, concat_axis=0, tiled=True)  10 us
    ppermute x4, starting transfers between devices, moved(): return lax.ppermute(x, axis, [(i, (i + step) % size) for i in range(size)])  8.6 us
    all_to_all x1, starting transfers between devices, on_device(): lax.all_to_all(request.reshape(nbatch, CAP * 2), BATCH, split_axis=0, con...  7.57 us
  transfers between devices with their start and end apart: 8, of which 6 were waited for; matrix products, arithmetic and copies ran while one was open for 2% of the time, Pallas kernels for 17%

profile of v4, /device:TPU:1, one launch (start us, length us, event | category | flops | bytes accessed | tf_op | source)
XLA Modules:
  0.0 173.4 jit_solution(4826481683231981838)
XLA Ops:
  0.6 0.8 copy.19
  2.0 1.3 route.1
  3.3 1.3 all_to_all.15
  4.6 7.6 %all-to-all-start = ((s32[16,1,4]{2,1,0:T(1,128)}), s32[16,1,4]{2,1,0:T(1,128)S(1)}, u32[]{:S(2)}, u32[]{:S(2)}) async-start(s32[16,1,4]{2,1,0:T(1,128)} %bitcast.1), calls=%async_computation | async-start | bytes 16384 | tf_op jit(solution)/shard_map/all_to_all | solution.py:614
  12.2 3.9 %pack.1 = bf16[32,256,256]{2,1,0:T(8,128)(2,1)} custom-call(s32[16]{0:T(128)} %get-tuple-element.19.slots, f32[16,256,256]{2,1,0:T(8,128)} %values.1), custom_call_target="tpu_custom_call" | custom-call | tf_op jit(solution)/shard_map/pack/pallas_call | solution.py:568
  16.1 2.5 %all-to-all-done = s32[16,1,4]{2,1,0:T(1,128)S(1)} async-done(((s32[16,1,4]{2,1,0:T(1,128)}), s32[16,1,4]{2,1,0:T(1,128)S(1)}, u32[]{:S(2)}, u32[]{:S(2)}) %all-to-all-start) | async-done | bytes 288 | tf_op jit(solution)/shard_map/all_to_all | solution.py:614
  18.6 4.5 %all-to-all-start.1 = ((bf16[16,2,256,256]{3,2,1,0:T(8,128)(2,1)}), bf16[16,2,256,256]{3,2,1,0:T(8,128)(2,1)}, u32[]{:S(2)}, u32[]{:S(2)}) async-start(bf16[16,2,256,256]{3,2,1,0:T(8,128)(2,1)} %bitcast.9), calls=%async_computation.1 | async-start | bytes 8388608 | tf_op jit(solution)/shard_map/all_to_all | solution.py:618
  24.9 20.4 %forward.1 = (f32[16,2,2,256,256]{4,3,2,1,0:T(8,128)}, bf16[16,2,2,256,256]{4,3,2,1,0:T(8,128)(2,1)}, f32[8,384]{1,0:T(8,128)}, f32[8,384]{1,0:T(8,128)}) custom-call(s32[64]{0:T(128)} %reshape.36.wanted, f32[2,2,384,384]{3,2,1,0:T(8,128)} %tile.1, bf16[2,256,256]{2,1,0:T(8,128)(2,1)} %probe.3, bf16[3,256,256]{2,1,0:T(8,128)(2,1)} %constant.11.clone.tab, ...), custom_call_target="tpu_custom_call" | custom-call | flops 25769803776 | bytes 33554432 | tf_op jit(solution)/shard_map/forward/pallas_call | solution.py:472
  45.3 0.8 fusion.1
  46.1 6.8 %collective-permute-start.1 = (f32[4,384]{1,0:T(4,128)S(1)}, f32[4,384]{1,0:T(4,128)S(1)}, u32[]{:S(2)}, u32[]{:S(2)}) collective-permute-start(f32[4,384]{1,0:T(4,128)S(1)} %get-tuple-element.34), channel_id=1, source_target_pairs={{0,120},{8,0},{16,8},{24,16},{32,24},{40,32},{48,40},{56,48},{64,5... | collective-permute-start | bytes 18440 | tf_op jit(solution)/shard_map/ppermute | solution.py:586
  52.9 0.8 fusion
  53.7 25.9 %collective-permute-done.1 = f32[4,384]{1,0:T(4,128)S(1)} collective-permute-done((f32[4,384]{1,0:T(4,128)S(1)}, f32[4,384]{1,0:T(4,128)S(1)}, u32[]{:S(2)}, u32[]{:S(2)}) %collective-permute-start.1) | collective-permute-done | bytes 6176 | tf_op jit(solution)/shard_map/ppermute | solution.py:586
  80.0 2.6 %all-to-all-done.1 = bf16[16,2,256,256]{3,2,1,0:T(8,128)(2,1)} async-done(((bf16[16,2,256,256]{3,2,1,0:T(8,128)(2,1)}), bf16[16,2,256,256]{3,2,1,0:T(8,128)(2,1)}, u32[]{:S(2)}, u32[]{:S(2)}) %all-to-all-start.1) | async-done | bytes 4194336 | tf_op jit(solution)/shard_map/all_to_all | solution.py:618
  82.6 25.1 %backward.1 = (f32[2,2,384,384]{3,2,1,0:T(8,128)}, bf16[128,8,128]{2,1,0:T(8,128)(2,1)}) custom-call(s32[64]{0:T(128)} %reshape.36.wanted, f32[2,2,384,384]{3,2,1,0:T(8,128)} %tile.1, bf16[2,256,256]{2,1,0:T(8,128)(2,1)} %probe.3, bf16[3,256,256]{2,1,0:T(8,128)(2,1)} %constant.11.clone.tab, f32[2,256,256]{2,1,0:T(8,128)} %constant.12.clone.prop, ...), custom_call_target="tpu_custom_call" | custom-call | flops 25769803776 | bytes 33554432 | tf_op jit(solution)/shard_map/backward/pallas_call | solution.py:490
  107.7 31.6 %all-to-all-start.2 = ((bf16[128,8,128]{2,1,0:T(8,128)(2,1)}), bf16[128,8,128]{2,1,0:T(8,128)(2,1)S(1)}, u32[]{:S(2)}, u32[]{:S(2)}) async-start(bf16[128,8,128]{2,1,0:T(8,128)(2,1)} %get-tuple-element.22), calls=%async_computation.2 | async-start | bytes 524288 | tf_op jit(solution)/shard_map/all_to_all | solution.py:601
  139.3 1.1 collective-permute-start.2
  140.4 0.7 collective-permute-start.3
  141.1 1.8 %collective-permute-done.2 = f32[4,512]{1,0:T(4,128)S(1)} collective-permute-done((f32[4,512]{1,0:T(4,128)S(1)}, f32[4,512]{1,0:T(4,128)S(1)}, u32[]{:S(2)}, u32[]{:S(2)}) %collective-permute-start.2) | collective-permute-done | bytes 8224 | tf_op jit(solution)/shard_map/ppermute | solution.py:586
  143.7 1.7 copy-done.1
  145.3 5.0 %finish.1 = f32[2,2,384,384]{3,2,1,0:T(8,128)} custom-call(f32[2,2,384,384]{3,2,1,0:T(8,128)S(1)} %copy-done, f32[2,2,384,384]{3,2,1,0:T(8,128)S(1)} %copy-done.1, f32[8,384]{1,0:T(8,128)S(1)} %pad_maximum_fusion.1.edge_rows, f32[8,512]{1,0:T(8,128)S(1)} %pad_maximum_fusion.edge_cols), custom_call_target="tpu_custom_call" | custom-call | tf_op jit(solution)/shard_map/finish/pallas_call | solution.py:502
  150.4 0.7 broadcast_in_dim.24
  151.2 10.0 %all-to-all-start.3 = ((bf16[128,8,128]{2,1,0:T(8,128)(2,1)}), bf16[128,8,128]{2,1,0:T(8,128)(2,1)S(1)}, u32[]{:S(2)}, u32[]{:S(2)}) async-start(bf16[128,8,128]{2,1,0:T(8,128)(2,1)} %broadcast_in_dim.24), calls=%async_computation.3 | async-start | bytes 524288 | tf_op jit(solution)/shard_map/all_to_all | solution.py:607
  161.3 10.7 %all-to-all-done.3 = bf16[128,8,128]{2,1,0:T(8,128)(2,1)S(1)} async-done(((bf16[128,8,128]{2,1,0:T(8,128)(2,1)}), bf16[128,8,128]{2,1,0:T(8,128)(2,1)S(1)}, u32[]{:S(2)}, u32[]{:S(2)}) %all-to-all-start.3) | async-done | bytes 262176 | tf_op jit(solution)/shard_map/all_to_all | solution.py:607
  172.4 1.0 copy.23
  (25 shorter events, 4.1 us)
Async XLA Ops:
  4.6 13.9 %all-to-all-start = ((s32[16,1,4]{2,1,0:T(1,128)}), s32[16,1,4]{2,1,0:T(1,128)S(1)}, u32[]{:S(2)}, u32[]{:S(2)}) async-start(s32[16,1,4]{2,1,0:T(1,128)} %bitcast.1), calls=%async_computation | async-start | bytes 16384 | tf_op jit(solution)/shard_map/all_to_all | solution.py:614
  18.6 64.1 %all-to-all-start.1 = ((bf16[16,2,256,256]{3,2,1,0:T(8,128)(2,1)}), bf16[16,2,256,256]{3,2,1,0:T(8,128)(2,1)}, u32[]{:S(2)}, u32[]{:S(2)}) async-start(bf16[16,2,256,256]{3,2,1,0:T(8,128)(2,1)} %bitcast.9), calls=%async_computation.1 | async-start | bytes 8388608 | tf_op jit(solution)/shard_map/all_to_all | solution.py:618
  46.1 33.5 %collective-permute-start.1 = (f32[4,384]{1,0:T(4,128)S(1)}, f32[4,384]{1,0:T(4,128)S(1)}, u32[]{:S(2)}, u32[]{:S(2)}) collective-permute-start(f32[4,384]{1,0:T(4,128)S(1)} %get-tuple-element.34), channel_id=1, source_target_pairs={{0,120},{8,0},{16,8},{24,16},{32,24},{40,32},{48,40},{56,48},{64,5... | collective-permute-start | bytes 18440 | tf_op jit(solution)/shard_map/ppermute | solution.py:586
  53.7 26.1 %collective-permute-start = (f32[4,384]{1,0:T(4,128)S(1)}, f32[4,384]{1,0:T(4,128)S(1)}, u32[]{:S(2)}, u32[]{:S(2)}) collective-permute-start(f32[4,384]{1,0:T(4,128)S(1)} %get-tuple-element.35), channel_id=1, source_target_pairs={{0,8},{8,16},{16,24},{24,32},{32,40},{40,48},{48,56},{56,64},{64,7... | collective-permute-start | bytes 18440 | tf_op jit(solution)/shard_map/ppermute | solution.py:586
  82.6 61.0 %copy-start = (f32[2,2,384,384]{3,2,1,0:T(8,128)S(1)}, f32[2,2,384,384]{3,2,1,0:T(8,128)}, u32[]{:S(2)}) copy-start(f32[2,2,384,384]{3,2,1,0:T(8,128)} %tile.1) | copy-start | bytes 7077892
  107.7 53.5 %copy-start.2 = (bf16[2,256,256]{2,1,0:T(8,128)(2,1)S(1)}, bf16[2,256,256]{2,1,0:T(8,128)(2,1)}, u32[]{:S(2)}) copy-start(bf16[2,256,256]{2,1,0:T(8,128)(2,1)} %probe.3) | copy-start | bytes 786436
  107.7 42.5 %all-to-all-start.2 = ((bf16[128,8,128]{2,1,0:T(8,128)(2,1)}), bf16[128,8,128]{2,1,0:T(8,128)(2,1)S(1)}, u32[]{:S(2)}, u32[]{:S(2)}) async-start(bf16[128,8,128]{2,1,0:T(8,128)(2,1)} %get-tuple-element.22), calls=%async_computation.2 | async-start | bytes 524288 | tf_op jit(solution)/shard_map/all_to_all | solution.py:601
  139.3 3.6 %collective-permute-start.2 = (f32[4,512]{1,0:T(4,128)S(1)}, f32[4,512]{1,0:T(4,128)S(1)}, u32[]{:S(2)}, u32[]{:S(2)}) collective-permute-start(f32[4,512]{1,0:T(4,128)S(1)} %get-tuple-element.24), channel_id=1, source_target_pairs={{0,7},{1,0},{2,1},{3,2},{4,3},{5,4},{6,5},{7,6},{8,15},{9,8},{10,9... | collective-permute-start | bytes 24584 | tf_op jit(solution)/shard_map/ppermute | solution.py:586
  140.4 3.2 %collective-permute-start.3 = (f32[4,512]{1,0:T(4,128)S(1)}, f32[4,512]{1,0:T(4,128)S(1)}, u32[]{:S(2)}, u32[]{:S(2)}) collective-permute-start(f32[4,512]{1,0:T(4,128)S(1)} %get-tuple-element.25), channel_id=1, source_target_pairs={{0,1},{1,2},{2,3},{3,4},{4,5},{5,6},{6,7},{7,0},{8,9},{9,10},{10,1... | collective-permute-start | bytes 24584 | tf_op jit(solution)/shard_map/ppermute | solution.py:586
  143.7 1.7 copy-start.1
  151.2 20.9 %all-to-all-start.3 = ((bf16[128,8,128]{2,1,0:T(8,128)(2,1)}), bf16[128,8,128]{2,1,0:T(8,128)(2,1)S(1)}, u32[]{:S(2)}, u32[]{:S(2)}) async-start(bf16[128,8,128]{2,1,0:T(8,128)(2,1)} %broadcast_in_dim.24), calls=%async_computation.3 | async-start | bytes 524288 | tf_op jit(solution)/shard_map/all_to_all | solution.py:607
